TPU v7x, 32 devices: a whole 2x2x4 slice. The times are simulated.
32 devices in a mesh: chord: 4 (over z), span: 8 (over y, x, core).
Axes of the slice: x: 2, y: 2, z: 4, core: 2. Of those that a mesh axis runs over, the one named last changes fastest.
Arguments:
- state: float32 [5, 125, 16, 16, 128], P(None, None, 'chord', 'span'), may hold values from -10 to 10
Outputs:
- residual: float32 [5, 125, 16, 16, 128], P(None, None, 'chord', 'span')
- viscosity: float32 [125, 16, 16, 128], P(None, 'chord', 'span')
All inputs are finite; a program needn't handle non-finite values.
Results may differ from a plain program's by a relative error of at most 0.0001.
Values sent between devices are 32-bit elements; how exact they have to be, the bound alone decides.
A program may use at most 128 MiB of HBM per device.

v0:
```python
import functools
import math

import jax
import jax.numpy as jnp
import numpy as np
from jax import lax
from jax.experimental import pallas as pl
from jax.experimental.pallas import tpu as pltpu
from jax.sharding import PartitionSpec as P

VMEM_BYTES = 52_500_000
EPS_SCALE = 0.01
SENSOR_CENTRE = -3.0
SENSOR_WIDTH = 1.5
RATIO_FLOOR = 1e-06
ENERGY_EPS = 1e-06
GAUSS_NODES = [-0.906179845938664, -0.5384693101056831, 0.0, 0.5384693101056831, 0.906179845938664]
GAUSS_WEIGHTS = [
    0.2369268850561891,
    0.4786286704993665,
    0.5688888888888889,
    0.4786286704993665,
    0.2369268850561891,
]


def legendre_values(points):
    values = [np.ones(points.shape), np.array(points)]
    for order in range(1, 5):
        values.append(
            ((2 * order + 1) * points * values[order] - order * values[order - 1]) / (order + 1)
        )
    return values


def line_tables():
    line_nodes = np.array(GAUSS_NODES)
    quadrature_weights = np.array(GAUSS_WEIGHTS)
    barycentric = np.array(
        [
            1.0 / np.prod([line_nodes[j] - line_nodes[k] for k in range(5) if k != j])
            for j in range(5)
        ]
    )
    derivative = np.zeros((5, 5))
    for i in range(5):
        for j in range(5):
            if i != j:
                derivative[i, j] = barycentric[j] / barycentric[i] / (line_nodes[i] - line_nodes[j])
        derivative[i, i] = -np.sum(derivative[i])
    left_values = np.ones(5)
    right_values = np.ones(5)
    for j in range(5):
        for k in range(5):
            if k != j:
                left_values[j] *= (-1.0 - line_nodes[k]) / (line_nodes[j] - line_nodes[k])
                right_values[j] *= (1.0 - line_nodes[k]) / (line_nodes[j] - line_nodes[k])
    legendre = legendre_values(line_nodes)
    fourth_slope = 7.0 * legendre[3] + 3.0 * legendre[1]
    fifth_slope = 9.0 * legendre[4] + 5.0 * legendre[2] + legendre[0]
    left_corr = 0.5 * (fourth_slope - fifth_slope)
    right_corr = 0.5 * (fourth_slope + fifth_slope)
    modal = np.zeros((5, 5))
    for k in range(5):
        modal[k, :] = quadrature_weights * math.sqrt((2 * k + 1) / 2.0) * legendre[k]
    return (line_nodes, derivative, left_values, right_values, left_corr, right_corr, modal)


NODES, DERIV, LEFT, RIGHT, LIFT_LEFT, LIFT_RIGHT, MODAL = line_tables()
HALF_LEFT = 0.5 * LIFT_LEFT
HALF_RIGHT = 0.5 * LIFT_RIGHT


def fold(u):
    return (u[0] + u[4], u[1] + u[3], u[2], u[0] - u[4], u[1] - u[3])


def traces(parts):
    s0, s1, mid, d0, d1 = parts
    r = [float(x) for x in RIGHT]
    even = 0.5 * (r[0] + r[4]) * s0 + 0.5 * (r[1] + r[3]) * s1 + r[2] * mid
    odd = 0.5 * (r[0] - r[4]) * d0 + 0.5 * (r[1] - r[3]) * d1
    return even - odd, even + odd


def slope(parts, before, after):
    s0, s1, mid, d0, d1 = parts
    h = [float(x) for x in HALF_LEFT]
    r = [float(x) for x in RIGHT]
    if before is not None:
        diff, both = before - after, before + after
    even, odd = [], []
    for i in range(3):
        lift = 0.5 * (h[i] + h[4 - i])
        value = (
            float(0.5 * (DERIV[i, 0] - DERIV[i, 4]) + lift * (r[0] - r[4])) * d0
            + float(0.5 * (DERIV[i, 1] - DERIV[i, 3]) + lift * (r[1] - r[3])) * d1
        )
        even.append(value if before is None else value + lift * diff)
    for i in range(2):
        lift = 0.5 * (h[i] - h[4 - i])
        value = (
            float(0.5 * (DERIV[i, 0] + DERIV[i, 4]) - lift * (r[0] + r[4])) * s0
            + float(0.5 * (DERIV[i, 1] + DERIV[i, 3]) - lift * (r[1] + r[3])) * s1
            + float(DERIV[i, 2] - 2.0 * lift * r[2]) * mid
        )
        odd.append(value if before is None else value + lift * both)
    return [even[0] + odd[0], even[1] + odd[1], even[2], even[1] - odd[1], even[0] - odd[0]]


def points(axis, q, j):
    if axis == 0:
        return [25 * i + 5 * q + j for i in range(5)]
    if axis == 1:
        return [25 * q + 5 * i + j for i in range(5)]
    return [25 * q + 5 * j + i for i in range(5)]


def modal_line(u):
    s0, s1, mid, d0, d1 = fold(u)
    out = []
    for k in range(5):
        m = [float(x) for x in MODAL[k]]
        out.append(m[0] * s0 + m[1] * s1 + m[2] * mid if k % 2 == 0 else m[0] * d0 + m[1] * d1)
    return out


def sensor(load, work):
    def first(q, carry):
        for j in range(5):
            pts = points(0, q, j)
            for i, value in zip(pts, modal_line([load(p) for p in pts])):
                work[i] = value
        return carry

    lax.fori_loop(0, 5, first, 0)

    def second(q, carry):
        total, high = carry
        plane = {}
        for c in range(5):
            for b, value in enumerate(modal_line([work[25 * q + 5 * b + c] for b in range(5)])):
                plane[b, c] = value
        low = jnp.zeros_like(total)
        edge = jnp.zeros_like(total)
        for b in range(5):
            line = modal_line([plane[b, c] for c in range(5)])
            squares = [x * x for x in line]
            if b < 4:
                low = low + ((squares[0] + squares[1]) + (squares[2] + squares[3]))
                edge = edge + squares[4]
            else:
                edge = edge + ((squares[0] + squares[1]) + (squares[2] + squares[3])) + squares[4]
        plane_total = low + edge
        return total + plane_total, high + jnp.where(q == 4, plane_total, edge)

    zero = jnp.zeros(work.shape[1:], jnp.float32)
    total, high = lax.fori_loop(0, 5, second, (zero, zero))
    level = jnp.log(jnp.maximum(high / (total + ENERGY_EPS), RATIO_FLOOR)) * (1.0 / math.log(10.0))
    ramp = jnp.clip((level - SENSOR_CENTRE) / SENSOR_WIDTH, -1.0, 1.0)
    return EPS_SCALE * 0.5 * (1.0 + jnp.sin(0.5 * math.pi * ramp))


def rolled(value, shift, axis):
    size = value.shape[axis]
    return pltpu.roll(value, shift % size, axis)


LOWER = [float((1.0 - x) / 2.0) for x in NODES]
UPPER = [float((1.0 + x) / 2.0) for x in NODES]


def along_lanes(line):
    lanes = line.shape[1]
    lane = lax.broadcasted_iota(jnp.int32, line.shape, 1)
    before = jnp.where(lane == 0, 0.0, rolled(line, 1, 1))
    after = jnp.where(lane == lanes - 1, 0.0, rolled(line, -1, 1))
    return jnp.maximum(line, before), jnp.maximum(line, after)


def interpolate(neighbours, nu):
    corner = {}
    for x in range(2):
        for y in range(2):
            line = jnp.maximum(
                jnp.maximum(neighbours[x][y], neighbours[x + 1][y]),
                jnp.maximum(neighbours[x][y + 1], neighbours[x + 1][y + 1]),
            )
            corner[x, y, 0], corner[x, y, 1] = along_lanes(line)
    lower, upper = LOWER, UPPER
    for a in range(5):
        face = {
            (y, z): lower[a] * corner[0, y, z] + upper[a] * corner[1, y, z]
            for y in range(2)
            for z in range(2)
        }
        for b in range(5):
            edge = [lower[b] * face[0, z] + upper[b] * face[1, z] for z in range(2)]
            for c in range(5):
                nu[25 * a + 5 * b + c] = lower[c] * edge[0] + upper[c] * edge[1]
    return corner


def row_masks(axis, chords, spans, lanes):
    row = lax.broadcasted_iota(jnp.int32, (chords * spans, lanes), 0)
    if axis == 0:
        return row < spans, row >= (chords - 1) * spans
    place = row % spans
    return place == 0, place == spans - 1


def outer_rows(axis, chords, spans, last):
    if axis == 0:
        return pl.ds((chords - 1) * spans if last else 0, spans)
    return pl.ds(spans - 1 if last else 0, chords, spans)


def store_pair(work, slot, left, right, down, up, index, rows_low, rows_high):
    work[2 * slot] = left
    work[2 * slot + 1] = right
    down[index] = work[2 * slot, rows_low]
    up[index] = work[2 * slot + 1, rows_high]


def local_kernel(sizes, count, chords, spans, *refs):
    state_hbm = refs[0]
    nu, acc = refs[1:3]
    (
        state, grad, around, work, eps_out, faces_c, faces_s, gain, edge, beta, outside, alpha,
        t0, t1, t2, t3, f0, f1, f2, f3,
    ) = refs[3:23]
    ghosts, flux_ghosts = refs[23:27], refs[27:31]
    load_sem, eps_send, eps_recv, send_sem, recv_sem = refs[31:]
    sends = ((t0, t1, t2, t3), (f0, f1, f2, f3))
    lands = (ghosts, flux_ghosts)
    rows, lanes = nu.shape[1:]
    chord_size, span_size = sizes
    me_c, me_s = lax.axis_index("chord"), lax.axis_index("span")
    mesh_id = pl.DeviceIdType.MESH

    def load(v):
        return pltpu.make_async_copy(state_hbm.at[v], state.at[v], load_sem.at[v])

    for v in range(count):
        load(v).start()

    def reachable(dx):
        if dx == 0:
            return None
        return me_c + 1 < chord_size if dx == 1 else me_c > 0

    def guarded(cond, run):
        if cond is None:
            run()
        else:
            pl.when(cond)(run)

    def partner(dx, dy):
        return (me_c + dx, lax.rem(me_s + dy + span_size, span_size))

    offsets = [(dx, dy) for dx in (0, -1, 1) for dy in (-1, 0, 1) if (dx, dy) != (0, 0)]
    barrier = pltpu.get_barrier_semaphore()
    for dx, dy in offsets:

        def greet(dx=dx, dy=dy):
            pl.semaphore_signal(barrier, inc=1, device_id=partner(dx, dy), device_id_type=mesh_id)

        guarded(reachable(dx), greet)

    def eps_copy(dx, dy):
        slot = 3 * (dx + 1) + dy + 1
        return pltpu.make_async_remote_copy(
            src_ref=eps_out, dst_ref=around.at[1 - dx, 1 - dy],
            send_sem=eps_send.at[slot], recv_sem=eps_recv.at[8 - slot],
            device_id=partner(dx, dy), device_id_type=mesh_id,
        )

    ways = ((1, 0), (-1, 0), (0, 1), (0, -1))

    def message(stage, k, v):
        dx, dy = ways[k]
        return pltpu.make_async_remote_copy(
            src_ref=sends[stage][k].at[v], dst_ref=lands[stage][k].at[v],
            send_sem=send_sem.at[stage, k, v], recv_sem=recv_sem.at[stage, k, v],
            device_id=partner(dx, dy), device_id_type=mesh_id,
        )

    def launch(stage, axis, v):
        for k in (2 * axis, 2 * axis + 1):
            guarded(reachable(ways[k][0]), lambda k=k: message(stage, k, v).start())

    masks = [row_masks(axis, chords, spans, lanes) for axis in range(2)]
    outer = [[outer_rows(axis, chords, spans, last) for last in (False, True)] for axis in range(2)]

    def send_traces(axis, v):
        up, down = sends[0][2 * axis], sends[0][2 * axis + 1]
        faces = (faces_c, faces_s)[axis]

        def body(q, carry):
            for j in range(5):
                left, right = traces(fold([state[v, p] for p in points(axis, q, j)]))
                faces[v, 5 * q + j] = jnp.where(masks[axis][0], left, right)
                store_pair(work, j, left, right, down, up, (v, 5 * q + j), *outer[axis])
            return carry

        lax.fori_loop(0, 5, body, 0)

    load(0).wait()
    send_traces(1, 0)
    sides = jnp.where(me_c > 0, 1, 0) + jnp.where(me_c + 1 < chord_size, 1, 0)
    pl.semaphore_wait(barrier, 2 + 3 * sides)
    launch(0, 1, 0)
    eps = sensor(lambda p: state[0, p], work)
    eps_out[...] = eps
    around[1, 1] = eps
    for dx, dy in offsets:
        guarded(reachable(dx), lambda dx=dx, dy=dy: eps_copy(dx, dy).start())

    send_traces(0, 0)
    launch(0, 0, 0)

    def later_traces(v, carry):
        load(v).wait()
        for axis in (1, 0):
            send_traces(axis, v)
            launch(0, axis, v)
        return carry

    lax.fori_loop(1, count, later_traces, 0)

    lane = lax.broadcasted_iota(jnp.int32, (rows, lanes), 1)
    first, last = lane == 0, lane == lanes - 1

    def normal_gradient(v, carry):
        def body(q, carry):
            for j in range(5):
                pts = points(2, q, j)
                parts = fold([state[v, p] for p in pts])
                left, right = traces(parts)
                before = jnp.where(first, left, rolled(right, 1, 1))
                after = jnp.where(last, right, rolled(left, -1, 1))
                for p, value in zip(pts, slope(parts, before, after)):
                    grad[v, p] = value
            return carry

        lax.fori_loop(0, 5, body, 0, unroll=True)
        return carry

    lax.fori_loop(0, count, normal_gradient, 0)

    row = lax.broadcasted_iota(jnp.int32, (rows, lanes), 0)
    for dx, dy in offsets:
        guarded(reachable(-dx), lambda dx=dx, dy=dy: eps_copy(dx, dy).wait_recv())

    have_low = jnp.where(me_c > 0, spans, 0)
    have_high = jnp.where(me_c + 1 < chord_size, rows, rows - spans)
    low_s, high_s = masks[1]
    low_c, high_c = masks[0]
    column = []
    for x in range(3):
        mine, left, right = around[x, 1], around[x, 0], around[x, 2]
        column.append([
            jnp.where(low_s, rolled(left, 1 - spans, 0), rolled(mine, 1, 0)),
            mine,
            jnp.where(high_s, rolled(right, spans - 1, 0), rolled(mine, -1, 0)),
            jnp.where(low_s, rolled(left, 2 - spans, 0), rolled(right, spans - 2, 0)),
        ])
    closed_low = row < spans - have_low
    closed_high = row >= have_high
    neighbours = [[], [], [], []]
    for y in range(4):
        inner = column[1][y]
        below = jnp.where(low_c, rolled(column[0][y], spans, 0), rolled(inner, spans, 0))
        above = jnp.where(high_c, rolled(column[2][y], -spans, 0), rolled(inner, -spans, 0))
        beyond = jnp.where(
            low_c, rolled(column[0][y], 2 * spans, 0), rolled(column[2][y], -2 * spans, 0)
        )
        neighbours[0].append(jnp.where(closed_low, 0.0, below))
        neighbours[1].append(inner)
        neighbours[2].append(jnp.where(closed_high, 0.0, above))
        neighbours[3].append(beyond)
    corner = interpolate(neighbours, nu)
    near_weight = sum(float(LEFT[i] * HALF_LEFT[i] * (1.0 - NODES[i]) / 2.0) for i in range(5))
    far_weight = sum(float(LEFT[i] * HALF_LEFT[i] * (1.0 + NODES[i]) / 2.0) for i in range(5))
    for axis in range(2):
        low = masks[axis][0]
        sign = jnp.where(low, -1.0, 1.0)
        weight = {}
        for t in range(2):
            pair = []
            for o in (t, t + 1):
                if axis == 0:
                    pair += [jnp.where(low, neighbours[0][o], neighbours[2][o]), neighbours[3][o]]
                else:
                    pair += [jnp.where(low, neighbours[o][0], neighbours[o][2]), neighbours[o][3]]
            line = jnp.maximum(jnp.maximum(pair[0], pair[1]), jnp.maximum(pair[2], pair[3]))
            far = along_lanes(line)
            for z in range(2):
                if axis == 0:
                    near = jnp.where(low, corner[0, t, z], corner[1, t, z])
                else:
                    near = jnp.where(low, corner[t, 0, z], corner[t, 1, z])
                weight[t, z] = sign * (near_weight * near + far_weight * far[z])
        for m in range(5):
            ends = [LOWER[m] * weight[0, z] + UPPER[m] * weight[1, z] for z in range(2)]
            for c in range(5):
                beta[axis, 5 * m + c] = LOWER[c] * ends[0] + UPPER[c] * ends[1]

    for axis in (1, 0):

        def variable(v, carry):
            up, down = sends[1][2 * axis], sends[1][2 * axis + 1]
            low, high = masks[axis]
            step = spans if axis == 0 else 1

            def body(q, carry):
                for j in range(5):
                    pts = points(axis, q, j)
                    parts = fold([state[v, p] for p in pts])
                    left, right = traces(parts)
                    before = jnp.where(low, 0.0, rolled(right, step, 0))
                    after = jnp.where(high, 0.0, rolled(left, -step, 0))
                    if axis == 0:
                        before = jnp.where(closed_low, left, before)
                        after = jnp.where(closed_high, right, after)
                    gradient = slope(parts, before, after)
                    parts = fold([nu[p] * g for p, g in zip(pts, gradient)])
                    left, right = traces(parts)
                    store_pair(work, j, left, right, down, up, (v, 5 * q + j), *outer[axis])
                    before = jnp.where(low, 0.0, rolled(right, step, 0))
                    after = jnp.where(high, 0.0, rolled(left, -step, 0))
                    if axis == 0:
                        before = jnp.where(closed_low, -left, before)
                        after = jnp.where(closed_high, -right, after)
                    for p, value in zip(pts, slope(parts, before, after)):
                        if axis == 1:
                            acc[v, p] = value
                        else:
                            acc[v, p] += value
                return carry

            lax.fori_loop(0, 5, body, 0, unroll=True)
            launch(1, axis, v)
            return carry

        lax.fori_loop(0, count, variable, 0)

    for axis in range(2):
        low, high = masks[axis]

        def gains(q, carry):
            for j in range(5):
                f = 5 * q + j
                spread = []
                for i, p in enumerate(points(axis, q, j)):
                    lift = jnp.where(high, float(HALF_RIGHT[i]), 0.0)
                    spread.append(nu[p] * jnp.where(low, float(HALF_LEFT[i]), lift))
                parts = fold(spread)
                left, right = traces(parts)
                edge[axis, 2 * f] = left
                edge[axis, 2 * f + 1] = right
                for i, value in enumerate(slope(parts, None, None)):
                    gain[axis, 5 * f + i] = value
            return carry

        lax.fori_loop(0, 5, gains, 0)

    def normal(v, carry):
        def body(q, carry):
            for j in range(5):
                pts = points(2, q, j)
                parts = fold([nu[p] * grad[v, p] for p in pts])
                left, right = traces(parts)
                before = jnp.where(first, -left, rolled(right, 1, 1))
                after = jnp.where(last, -right, rolled(left, -1, 1))
                for p, value in zip(pts, slope(parts, before, after)):
                    acc[v, p] += value
            return carry

        lax.fori_loop(0, 5, body, 0, unroll=True)
        return carry

    lax.fori_loop(0, count, normal, 0)

    def arrived(axis, v):
        for k in (2 * axis, 2 * axis + 1):
            for stage in range(2):
                guarded(
                    reachable(-ways[k][0]),
                    lambda k=k, stage=stage: message(stage, k, v).wait_recv(),
                )

    for axis in (0, 1):

        def correct(v, carry):
            arrived(axis, v)
            up, down = ghosts[2 * axis], ghosts[2 * axis + 1]
            f_up, f_down = flux_ghosts[2 * axis], flux_ghosts[2 * axis + 1]
            faces = (faces_c, faces_s)[axis]
            low, high = masks[axis]
            rows_low, rows_high = outer[axis]
            step = spans if axis == 0 else 1
            opened = low | high
            if axis == 0:
                opened = opened & jnp.logical_not(closed_low | closed_high)

            def gather(q, carry):
                for j in range(5):
                    f = 5 * q + j
                    outside[f, rows_low] = up[v, f]
                    outside[f, rows_high] = down[v, f]
                    alpha[f, rows_low] = f_up[v, f]
                    alpha[f, rows_high] = f_down[v, f]
                return carry

            lax.fori_loop(0, 5, gather, 0)

            def body(q, carry):
                for j in range(5):
                    f = 5 * q + j
                    ghost = jnp.where(opened, outside[f], 0.0)
                    flux = jnp.where(opened, alpha[f] + beta[axis, f] * faces[v, f], 0.0)
                    before = jnp.where(low, flux, rolled(edge[axis, 2 * f + 1] * ghost, step, 0))
                    after = jnp.where(high, flux, rolled(edge[axis, 2 * f] * ghost, -step, 0))
                    h = [float(x) for x in HALF_LEFT]
                    diff, both = before - after, before + after
                    even = [0.5 * (h[i] + h[4 - i]) * diff for i in range(3)]
                    odd = [0.5 * (h[i] - h[4 - i]) * both for i in range(2)]
                    lifts = [
                        even[0] + odd[0], even[1] + odd[1], even[2],
                        even[1] - odd[1], even[0] - odd[0],
                    ]
                    for i, p in enumerate(points(axis, q, j)):
                        acc[v, p] += gain[axis, 5 * f + i] * ghost + lifts[i]
                return carry

            lax.fori_loop(0, 5, body, 0, unroll=True)
            return carry

        lax.fori_loop(0, count, correct, 0)

    for dx, dy in offsets:
        guarded(reachable(dx), lambda dx=dx, dy=dy: eps_copy(dx, dy).wait_send())
    for stage in range(2):
        for k in range(4):
            for v in range(count):
                guarded(
                    reachable(ways[k][0]),
                    lambda stage=stage, k=k, v=v: message(stage, k, v).wait_send(),
                )


def shards(state):
    count, npts, chords, spans, lanes = state.shape
    rows = chords * spans
    flat = state.reshape(count, npts, rows, lanes)
    f32 = jnp.float32
    sizes = (lax.axis_size("chord"), lax.axis_size("span"))

    def message(n, k):
        return (n, 25, spans if k < 2 else chords, lanes)

    def full(*shape):
        return jax.ShapeDtypeStruct(shape, f32)

    vmem = pl.BlockSpec(memory_space=pltpu.VMEM)
    nu, residual = pl.pallas_call(
        functools.partial(local_kernel, sizes, count, chords, spans),
        in_specs=[pl.BlockSpec(memory_space=pltpu.HBM)],
        out_specs=[vmem, vmem],
        out_shape=[full(npts, rows, lanes), full(count, npts, rows, lanes)],
        scratch_shapes=[
            pltpu.VMEM(shape, f32)
            for shape in [
                (count, npts, rows, lanes),
                (count, npts, rows, lanes),
                (3, 3, rows, lanes),
                (npts, rows, lanes),
                (rows, lanes),
                (count, 25, rows, lanes),
                (count, 25, rows, lanes),
                (2, npts, rows, lanes),
                (2, 50, rows, lanes),
                (2, 25, rows, lanes),
                (25, rows, lanes),
                (25, rows, lanes),
            ]
            + [message(count, k) for k in range(4)] * 4
        ]
        + [
            pltpu.SemaphoreType.DMA((count,)),
            pltpu.SemaphoreType.DMA((9,)),
            pltpu.SemaphoreType.DMA((9,)),
            pltpu.SemaphoreType.DMA((2, 4, count)),
            pltpu.SemaphoreType.DMA((2, 4, count)),
        ],
        compiler_params=pltpu.CompilerParams(
            collective_id=0, has_side_effects=True, vmem_limit_bytes=VMEM_BYTES
        ),
    )(flat)
    return residual.reshape(state.shape), nu.reshape(npts, chords, spans, lanes)


def solution(mesh):
    in_specs = (P(None, None, "chord", "span", None),)
    out_specs = (P(None, None, "chord", "span", None), P(None, "chord", "span", None))
    return jax.shard_map(shards, mesh=mesh, in_specs=in_specs, out_specs=out_specs, check_vma=False)
```

profile of v0, /device:TPU:0, one launch (start us, length us, event | category | flops | bytes accessed | tf_op | source)
XLA Modules:
  0.0 21.6 jit_solution(18401190923153131121)
XLA Ops:
  0.6 18.7 %shard_map.30 = (f32[125,8,128]{2,1,0:T(8,128)S(1)}, f32[5,125,8,128]{3,2,1,0:T(8,128)S(1)}) custom-call(f32[5,125,8,128]{3,2,1,0:T(8,128)} %bitcast.5), custom_call_target="tpu_custom_call" | custom-call | tf_op jit(solution)/shard_map/pallas_call | solution.py:568
  19.3 1.5 %copy.5 = f32[5,125,4,2,128]{4,3,2,1,0:T(2,128)} copy(f32[5,125,4,2,128]{4,3,2,1,0:T(2,128)S(1)} %bitcast.3) | data formatting | bytes 5120000
  20.8 0.8 %copy.6 = f32[125,4,2,128]{3,2,1,0:T(2,128)} copy(f32[125,4,2,128]{3,2,1,0:T(2,128)S(1)} %bitcast.4) | data formatting | bytes 1024000
where the time goes:
time: 21.7 us; the launch traced here: 21.6 us
  Pallas kernels  18.7 us (86%)
  local copies, waits for them, and re-layouts  2.26 us (10%)
  between operations  0.64 us (3%)
    pallas_call x1, Pallas kernels, shards(): pl.pallas_call(functools.partial(local_kernel, sizes, count, chords, span...  18.7 us
    unnamed x2, local copies, waits for them, and re-layouts  2.26 us

commit v1 on v0

--- a/solution.py
+++ b/solution.py
@@ -10,6 +10,7 @@
 from jax.sharding import PartitionSpec as P
 
 VMEM_BYTES = 52_500_000
+FINISH_BYTES = 8_000_000
 EPS_SCALE = 0.01
 SENSOR_CENTRE = -3.0
 SENSOR_WIDTH = 1.5
@@ -551,6 +552,18 @@
                 )
 
 
+def finish_kernel(acc, nu, residual_out, nu_out, sems):
+    copies = [
+        pltpu.make_async_copy(acc.at[v], residual_out.at[v], sems.at[v])
+        for v in range(acc.shape[0])
+    ]
+    copies.append(pltpu.make_async_copy(nu, nu_out, sems.at[acc.shape[0]]))
+    for copy in copies:
+        copy.start()
+    for copy in copies:
+        copy.wait()
+
+
 def shards(state):
     count, npts, chords, spans, lanes = state.shape
     rows = chords * spans
@@ -599,6 +612,15 @@
             collective_id=0, has_side_effects=True, vmem_limit_bytes=VMEM_BYTES
         ),
     )(flat)
+    hbm = pl.BlockSpec(memory_space=pltpu.HBM)
+    residual, nu = pl.pallas_call(
+        finish_kernel,
+        in_specs=[vmem, vmem],
+        out_specs=[hbm, hbm],
+        out_shape=[full(count, npts, rows, lanes), full(npts, rows, lanes)],
+        scratch_shapes=[pltpu.SemaphoreType.DMA((count + 1,))],
+        compiler_params=pltpu.CompilerParams(vmem_limit_bytes=FINISH_BYTES),
+    )(residual, nu)
     return residual.reshape(state.shape), nu.reshape(npts, chords, spans, lanes)
 
 

time: 21.7 us -> 21.2 us (0.977)
  local copies, waits for them, and re-layouts: 2.26 us -> 0 us
  Pallas kernels: 18.7 us -> 20.4 us
    unnamed x2 -> x0, local copies, waits for them, and re-layouts: 2.26 us -> none
    pallas_call x0 -> x1, Pallas kernels: none -> 1.68 us  [shards(): pl.pallas_call(finish_kernel, in_specs=[vmem, vmem], out_specs=[hbm, hbm]...]
where the time goes in v1:
time: 21.2 us; the launch traced here: 21 us
  Pallas kernels  20.4 us (96%)
  between operations  0.64 us (3%)
    pallas_call x1, Pallas kernels, shards(): pl.pallas_call(functools.partial(local_kernel, sizes, count, chords, span...  18.7 us
    pallas_call x1, Pallas kernels, shards(): pl.pallas_call(finish_kernel, in_specs=[vmem, vmem], out_specs=[hbm, hbm]...  1.68 us

profile of v1, /device:TPU:0, one launch (start us, length us, event | category | flops | bytes accessed | tf_op | source)
XLA Modules:
  0.0 21.0 jit_solution(679236438456340852)
XLA Ops:
  0.6 18.7 %shard_map.30 = (f32[125,8,128]{2,1,0:T(8,128)S(1)}, f32[5,125,8,128]{3,2,1,0:T(8,128)S(1)}) custom-call(f32[5,125,8,128]{3,2,1,0:T(8,128)} %bitcast.3), custom_call_target="tpu_custom_call" | custom-call | tf_op jit(solution)/shard_map/pallas_call | solution.py:581
  19.3 1.7 %shard_map.31 = (f32[5,125,8,128]{3,2,1,0:T(8,128)}, f32[125,8,128]{2,1,0:T(8,128)}) custom-call(f32[5,125,8,128]{3,2,1,0:T(8,128)S(1)} %get-tuple-element.6.acc, f32[125,8,128]{2,1,0:T(8,128)S(1)} %get-tuple-element.7.nu), custom_call_target="tpu_custom_call" | custom-call | tf_op jit(solution)/shard_map/pallas_call | solution.py:616

commit v2 on v1

--- a/solution.py
+++ b/solution.py
@@ -200,7 +200,6 @@
             edge = [lower[b] * face[0, z] + upper[b] * face[1, z] for z in range(2)]
             for c in range(5):
                 nu[25 * a + 5 * b + c] = lower[c] * edge[0] + upper[c] * edge[1]
-    return corner
 
 
 def row_masks(axis, chords, spans, lanes):
@@ -211,34 +210,27 @@
     return place == 0, place == spans - 1
 
 
-def outer_rows(axis, chords, spans, last):
-    if axis == 0:
-        return pl.ds((chords - 1) * spans if last else 0, spans)
-    return pl.ds(spans - 1 if last else 0, chords, spans)
-
-
-def store_pair(work, slot, left, right, down, up, index, rows_low, rows_high):
-    work[2 * slot] = left
-    work[2 * slot + 1] = right
-    down[index] = work[2 * slot, rows_low]
-    up[index] = work[2 * slot + 1, rows_high]
+def total_of(values):
+    out = values[0]
+    for value in values[1:]:
+        out = out + value
+    return out
 
 
 def local_kernel(sizes, count, chords, spans, *refs):
     state_hbm = refs[0]
     nu, acc = refs[1:3]
-    (
-        state, grad, around, work, eps_out, faces_c, faces_s, gain, edge, beta, outside, alpha,
-        t0, t1, t2, t3, f0, f1, f2, f3,
-    ) = refs[3:23]
-    ghosts, flux_ghosts = refs[23:27], refs[27:31]
-    load_sem, eps_send, eps_recv, send_sem, recv_sem = refs[31:]
-    sends = ((t0, t1, t2, t3), (f0, f1, f2, f3))
-    lands = (ghosts, flux_ghosts)
+    state, grad, around, work, eps_out = refs[3:8]
+    faces = (refs[8:10], refs[10:12])
+    ghosts = (refs[12:14], refs[14:16])
+    load_sem, eps_send, eps_recv, send_sem, recv_sem = refs[16:]
     rows, lanes = nu.shape[1:]
     chord_size, span_size = sizes
     me_c, me_s = lax.axis_index("chord"), lax.axis_index("span")
     mesh_id = pl.DeviceIdType.MESH
+
+    def whole(ref):
+        return ref.reshape(count, 25, rows, lanes)
 
     def load(v):
         return pltpu.make_async_copy(state_hbm.at[v], state.at[v], load_sem.at[v])
@@ -279,10 +271,17 @@
 
     ways = ((1, 0), (-1, 0), (0, 1), (0, -1))
 
+    def side(ref, axis, v, last):
+        if axis == 0:
+            return ref.at[v, :, chords - 1 if last else 0]
+        return ref.at[v, :, :, spans - 1 if last else 0]
+
     def message(stage, k, v):
         dx, dy = ways[k]
+        axis, up = k // 2, k % 2 == 0
         return pltpu.make_async_remote_copy(
-            src_ref=sends[stage][k].at[v], dst_ref=lands[stage][k].at[v],
+            src_ref=side(faces[stage][axis], axis, v, up),
+            dst_ref=side(ghosts[stage][axis], axis, v, not up),
             send_sem=send_sem.at[stage, k, v], recv_sem=recv_sem.at[stage, k, v],
             device_id=partner(dx, dy), device_id_type=mesh_id,
         )
@@ -291,27 +290,30 @@
         for k in (2 * axis, 2 * axis + 1):
             guarded(reachable(ways[k][0]), lambda k=k: message(stage, k, v).start())
 
+    def arrived(stage, axis, v):
+        for k in (2 * axis, 2 * axis + 1):
+            guarded(reachable(-ways[k][0]), lambda k=k: message(stage, k, v).wait_recv())
+
+    def sent(stage, axis, v):
+        for k in (2 * axis, 2 * axis + 1):
+            guarded(reachable(ways[k][0]), lambda k=k: message(stage, k, v).wait_send())
+
     masks = [row_masks(axis, chords, spans, lanes) for axis in range(2)]
-    outer = [[outer_rows(axis, chords, spans, last) for last in (False, True)] for axis in range(2)]
 
     def send_traces(axis, v):
-        up, down = sends[0][2 * axis], sends[0][2 * axis + 1]
-        faces = (faces_c, faces_s)[axis]
-
-        def body(q, carry):
+        low = masks[axis][0]
+        ends = [jnp.where(low, float(LEFT[i]), float(RIGHT[i])) for i in range(5)]
+        out = whole(faces[0][axis])
+        for q in range(5):
             for j in range(5):
-                left, right = traces(fold([state[v, p] for p in points(axis, q, j)]))
-                faces[v, 5 * q + j] = jnp.where(masks[axis][0], left, right)
-                store_pair(work, j, left, right, down, up, (v, 5 * q + j), *outer[axis])
-            return carry
-
-        lax.fori_loop(0, 5, body, 0)
+                pts = points(axis, q, j)
+                out[v, 5 * q + j] = total_of([e * state[v, p] for e, p in zip(ends, pts)])
+        launch(0, axis, v)
 
     load(0).wait()
-    send_traces(1, 0)
     sides = jnp.where(me_c > 0, 1, 0) + jnp.where(me_c + 1 < chord_size, 1, 0)
     pl.semaphore_wait(barrier, 2 + 3 * sides)
-    launch(0, 1, 0)
+    send_traces(1, 0)
     eps = sensor(lambda p: state[0, p], work)
     eps_out[...] = eps
     around[1, 1] = eps
@@ -319,13 +321,11 @@
         guarded(reachable(dx), lambda dx=dx, dy=dy: eps_copy(dx, dy).start())
 
     send_traces(0, 0)
-    launch(0, 0, 0)
 
     def later_traces(v, carry):
         load(v).wait()
         for axis in (1, 0):
             send_traces(axis, v)
-            launch(0, axis, v)
         return carry
 
     lax.fori_loop(1, count, later_traces, 0)
@@ -334,7 +334,7 @@
     first, last = lane == 0, lane == lanes - 1
 
     def normal_gradient(v, carry):
-        def body(q, carry):
+        for q in range(5):
             for j in range(5):
                 pts = points(2, q, j)
                 parts = fold([state[v, p] for p in pts])
@@ -343,9 +343,6 @@
                 after = jnp.where(last, right, rolled(left, -1, 1))
                 for p, value in zip(pts, slope(parts, before, after)):
                     grad[v, p] = value
-            return carry
-
-        lax.fori_loop(0, 5, body, 0, unroll=True)
         return carry
 
     lax.fori_loop(0, count, normal_gradient, 0)
@@ -358,6 +355,9 @@
     have_high = jnp.where(me_c + 1 < chord_size, rows, rows - spans)
     low_s, high_s = masks[1]
     low_c, high_c = masks[0]
+    closed_low = row < spans - have_low
+    closed_high = row >= have_high
+    closed = closed_low | closed_high
     column = []
     for x in range(3):
         mine, left, right = around[x, 1], around[x, 0], around[x, 2]
@@ -365,110 +365,57 @@
             jnp.where(low_s, rolled(left, 1 - spans, 0), rolled(mine, 1, 0)),
             mine,
             jnp.where(high_s, rolled(right, spans - 1, 0), rolled(mine, -1, 0)),
-            jnp.where(low_s, rolled(left, 2 - spans, 0), rolled(right, spans - 2, 0)),
         ])
-    closed_low = row < spans - have_low
-    closed_high = row >= have_high
-    neighbours = [[], [], [], []]
-    for y in range(4):
+    neighbours = [[], [], []]
+    for y in range(3):
         inner = column[1][y]
         below = jnp.where(low_c, rolled(column[0][y], spans, 0), rolled(inner, spans, 0))
         above = jnp.where(high_c, rolled(column[2][y], -spans, 0), rolled(inner, -spans, 0))
-        beyond = jnp.where(
-            low_c, rolled(column[0][y], 2 * spans, 0), rolled(column[2][y], -2 * spans, 0)
-        )
         neighbours[0].append(jnp.where(closed_low, 0.0, below))
         neighbours[1].append(inner)
         neighbours[2].append(jnp.where(closed_high, 0.0, above))
-        neighbours[3].append(beyond)
-    corner = interpolate(neighbours, nu)
-    near_weight = sum(float(LEFT[i] * HALF_LEFT[i] * (1.0 - NODES[i]) / 2.0) for i in range(5))
-    far_weight = sum(float(LEFT[i] * HALF_LEFT[i] * (1.0 + NODES[i]) / 2.0) for i in range(5))
-    for axis in range(2):
-        low = masks[axis][0]
-        sign = jnp.where(low, -1.0, 1.0)
-        weight = {}
-        for t in range(2):
-            pair = []
-            for o in (t, t + 1):
-                if axis == 0:
-                    pair += [jnp.where(low, neighbours[0][o], neighbours[2][o]), neighbours[3][o]]
-                else:
-                    pair += [jnp.where(low, neighbours[o][0], neighbours[o][2]), neighbours[o][3]]
-            line = jnp.maximum(jnp.maximum(pair[0], pair[1]), jnp.maximum(pair[2], pair[3]))
-            far = along_lanes(line)
-            for z in range(2):
-                if axis == 0:
-                    near = jnp.where(low, corner[0, t, z], corner[1, t, z])
-                else:
-                    near = jnp.where(low, corner[t, 0, z], corner[t, 1, z])
-                weight[t, z] = sign * (near_weight * near + far_weight * far[z])
-        for m in range(5):
-            ends = [LOWER[m] * weight[0, z] + UPPER[m] * weight[1, z] for z in range(2)]
-            for c in range(5):
-                beta[axis, 5 * m + c] = LOWER[c] * ends[0] + UPPER[c] * ends[1]
+    interpolate(neighbours, nu)
 
     for axis in (1, 0):
+        low, high = masks[axis]
+        step = spans if axis == 0 else 1
+        shut = jnp.where(closed, -1.0, 0.0)
+        mine, ghost = whole(faces[0][axis]), whole(ghosts[0][axis])
+        out = whole(faces[1][axis])
 
         def variable(v, carry):
-            up, down = sends[1][2 * axis], sends[1][2 * axis + 1]
-            low, high = masks[axis]
-            step = spans if axis == 0 else 1
-
-            def body(q, carry):
+            arrived(0, axis, v)
+            for q in range(5):
                 for j in range(5):
+                    f = 5 * q + j
                     pts = points(axis, q, j)
                     parts = fold([state[v, p] for p in pts])
                     left, right = traces(parts)
-                    before = jnp.where(low, 0.0, rolled(right, step, 0))
-                    after = jnp.where(high, 0.0, rolled(left, -step, 0))
+                    beyond = ghost[v, f]
                     if axis == 0:
-                        before = jnp.where(closed_low, left, before)
-                        after = jnp.where(closed_high, right, after)
+                        beyond = jnp.where(closed, mine[v, f], beyond)
+                    before = jnp.where(low, beyond, rolled(right, step, 0))
+                    after = jnp.where(high, beyond, rolled(left, -step, 0))
                     gradient = slope(parts, before, after)
                     parts = fold([nu[p] * g for p, g in zip(pts, gradient)])
                     left, right = traces(parts)
-                    store_pair(work, j, left, right, down, up, (v, 5 * q + j), *outer[axis])
-                    before = jnp.where(low, 0.0, rolled(right, step, 0))
-                    after = jnp.where(high, 0.0, rolled(left, -step, 0))
-                    if axis == 0:
-                        before = jnp.where(closed_low, -left, before)
-                        after = jnp.where(closed_high, -right, after)
+                    ends = jnp.where(low, left, right)
+                    out[v, f] = ends
+                    beyond = shut * ends if axis == 0 else 0.0
+                    before = jnp.where(low, beyond, rolled(right, step, 0))
+                    after = jnp.where(high, beyond, rolled(left, -step, 0))
                     for p, value in zip(pts, slope(parts, before, after)):
                         if axis == 1:
                             acc[v, p] = value
                         else:
                             acc[v, p] += value
-                return carry
-
-            lax.fori_loop(0, 5, body, 0, unroll=True)
             launch(1, axis, v)
             return carry
 
         lax.fori_loop(0, count, variable, 0)
 
-    for axis in range(2):
-        low, high = masks[axis]
-
-        def gains(q, carry):
-            for j in range(5):
-                f = 5 * q + j
-                spread = []
-                for i, p in enumerate(points(axis, q, j)):
-                    lift = jnp.where(high, float(HALF_RIGHT[i]), 0.0)
-                    spread.append(nu[p] * jnp.where(low, float(HALF_LEFT[i]), lift))
-                parts = fold(spread)
-                left, right = traces(parts)
-                edge[axis, 2 * f] = left
-                edge[axis, 2 * f + 1] = right
-                for i, value in enumerate(slope(parts, None, None)):
-                    gain[axis, 5 * f + i] = value
-            return carry
-
-        lax.fori_loop(0, 5, gains, 0)
-
     def normal(v, carry):
-        def body(q, carry):
+        for q in range(5):
             for j in range(5):
                 pts = points(2, q, j)
                 parts = fold([nu[p] * grad[v, p] for p in pts])
@@ -477,79 +424,44 @@
                 after = jnp.where(last, -right, rolled(left, -1, 1))
                 for p, value in zip(pts, slope(parts, before, after)):
                     acc[v, p] += value
-            return carry
-
-        lax.fori_loop(0, 5, body, 0, unroll=True)
+        for axis in range(2):
+            sent(0, axis, v)
         return carry
 
     lax.fori_loop(0, count, normal, 0)
-
-    def arrived(axis, v):
-        for k in (2 * axis, 2 * axis + 1):
-            for stage in range(2):
-                guarded(
-                    reachable(-ways[k][0]),
-                    lambda k=k, stage=stage: message(stage, k, v).wait_recv(),
-                )
-
-    for axis in (0, 1):
-
-        def correct(v, carry):
-            arrived(axis, v)
-            up, down = ghosts[2 * axis], ghosts[2 * axis + 1]
-            f_up, f_down = flux_ghosts[2 * axis], flux_ghosts[2 * axis + 1]
-            faces = (faces_c, faces_s)[axis]
-            low, high = masks[axis]
-            rows_low, rows_high = outer[axis]
-            step = spans if axis == 0 else 1
-            opened = low | high
-            if axis == 0:
-                opened = opened & jnp.logical_not(closed_low | closed_high)
-
-            def gather(q, carry):
-                for j in range(5):
-                    f = 5 * q + j
-                    outside[f, rows_low] = up[v, f]
-                    outside[f, rows_high] = down[v, f]
-                    alpha[f, rows_low] = f_up[v, f]
-                    alpha[f, rows_high] = f_down[v, f]
-                return carry
-
-            lax.fori_loop(0, 5, gather, 0)
-
-            def body(q, carry):
-                for j in range(5):
-                    f = 5 * q + j
-                    ghost = jnp.where(opened, outside[f], 0.0)
-                    flux = jnp.where(opened, alpha[f] + beta[axis, f] * faces[v, f], 0.0)
-                    before = jnp.where(low, flux, rolled(edge[axis, 2 * f + 1] * ghost, step, 0))
-                    after = jnp.where(high, flux, rolled(edge[axis, 2 * f] * ghost, -step, 0))
-                    h = [float(x) for x in HALF_LEFT]
-                    diff, both = before - after, before + after
-                    even = [0.5 * (h[i] + h[4 - i]) * diff for i in range(3)]
-                    odd = [0.5 * (h[i] - h[4 - i]) * both for i in range(2)]
-                    lifts = [
-                        even[0] + odd[0], even[1] + odd[1], even[2],
-                        even[1] - odd[1], even[0] - odd[0],
-                    ]
-                    for i, p in enumerate(points(axis, q, j)):
-                        acc[v, p] += gain[axis, 5 * f + i] * ghost + lifts[i]
-                return carry
-
-            lax.fori_loop(0, 5, body, 0, unroll=True)
-            return carry
-
-        lax.fori_loop(0, count, correct, 0)
 
     for dx, dy in offsets:
         guarded(reachable(dx), lambda dx=dx, dy=dy: eps_copy(dx, dy).wait_send())
-    for stage in range(2):
-        for k in range(4):
-            for v in range(count):
-                guarded(
-                    reachable(ways[k][0]),
-                    lambda stage=stage, k=k, v=v: message(stage, k, v).wait_send(),
-                )
+
+    lifts = [
+        [
+            jnp.where(low, float(HALF_LEFT[i]), jnp.where(high, float(HALF_RIGHT[i]), 0.0))
+            for i in range(5)
+        ]
+        for low, high in masks
+    ]
+    edges = [(low | high) for low, high in masks]
+    edges[0] = edges[0] & jnp.logical_not(closed)
+
+    def correct(v, carry):
+        for axis in range(2):
+            arrived(1, axis, v)
+        for axis in range(2):
+            sent(1, axis, v)
+        flux_c, flux_s = whole(ghosts[1][0]), whole(ghosts[1][1])
+        for c in range(5):
+            along = [
+                [jnp.where(edges[0], flux_c[v, 5 * b + c], 0.0) for b in range(5)],
+                [jnp.where(edges[1], flux_s[v, 5 * a + c], 0.0) for a in range(5)],
+            ]
+            for a in range(5):
+                for b in range(5):
+                    acc[v, 25 * a + 5 * b + c] += (
+                        lifts[0][a] * along[0][b] + lifts[1][b] * along[1][a]
+                    )
+        return carry
+
+    lax.fori_loop(0, count, correct, 0)
 
 
 def finish_kernel(acc, nu, residual_out, nu_out, sems):
@@ -570,9 +482,6 @@
     flat = state.reshape(count, npts, rows, lanes)
     f32 = jnp.float32
     sizes = (lax.axis_size("chord"), lax.axis_size("span"))
-
-    def message(n, k):
-        return (n, 25, spans if k < 2 else chords, lanes)
 
     def full(*shape):
         return jax.ShapeDtypeStruct(shape, f32)
@@ -591,15 +500,8 @@
                 (3, 3, rows, lanes),
                 (npts, rows, lanes),
                 (rows, lanes),
-                (count, 25, rows, lanes),
-                (count, 25, rows, lanes),
-                (2, npts, rows, lanes),
-                (2, 50, rows, lanes),
-                (2, 25, rows, lanes),
-                (25, rows, lanes),
-                (25, rows, lanes),
             ]
-            + [message(count, k) for k in range(4)] * 4
+            + [(count, 25, chords, spans, lanes)] * 8
         ]
         + [
             pltpu.SemaphoreType.DMA((count,)),

time: 21.2 us -> 21.3 us (level)
  no operation moved by 1% of the time
where the time goes in v2:
time: 21.3 us; the launch traced here: 21.2 us
  Pallas kernels  20.6 us (97%)
  between operations  0.64 us (3%)
    pallas_call x1, Pallas kernels, shards(): pl.pallas_call(functools.partial(local_kernel, sizes, count, chords, span...  18.9 us
    pallas_call x1, Pallas kernels, shards(): pl.pallas_call(finish_kernel, in_specs=[vmem, vmem], out_specs=[hbm, hbm]...  1.68 us

profile of v2, /device:TPU:0, one launch (start us, length us, event | category | flops | bytes accessed | tf_op | source)
XLA Modules:
  0.0 21.2 jit_solution(13623481261251665363)
XLA Ops:
  0.6 18.9 %shard_map.30 = (f32[125,8,128]{2,1,0:T(8,128)S(1)}, f32[5,125,8,128]{3,2,1,0:T(8,128)S(1)}) custom-call(f32[5,125,8,128]{3,2,1,0:T(8,128)} %bitcast.3), custom_call_target="tpu_custom_call" | custom-call | tf_op jit(solution)/shard_map/pallas_call | solution.py:490
  19.5 1.7 %shard_map.31 = (f32[5,125,8,128]{3,2,1,0:T(8,128)}, f32[125,8,128]{2,1,0:T(8,128)}) custom-call(f32[5,125,8,128]{3,2,1,0:T(8,128)S(1)} %get-tuple-element.6.acc, f32[125,8,128]{2,1,0:T(8,128)S(1)} %get-tuple-element.7.nu), custom_call_target="tpu_custom_call" | custom-call | tf_op jit(solution)/shard_map/pallas_call | solution.py:518

commit v3 on v2

--- a/solution.py
+++ b/solution.py
@@ -223,7 +223,7 @@
     state, grad, around, work, eps_out = refs[3:8]
     faces = (refs[8:10], refs[10:12])
     ghosts = (refs[12:14], refs[14:16])
-    load_sem, eps_send, eps_recv, send_sem, recv_sem = refs[16:]
+    load_sem, eps_sem, send_sem, state_sem, flux_sem, chord_sem = refs[16:]
     rows, lanes = nu.shape[1:]
     chord_size, span_size = sizes
     me_c, me_s = lax.axis_index("chord"), lax.axis_index("span")
@@ -232,11 +232,14 @@
     def whole(ref):
         return ref.reshape(count, 25, rows, lanes)
 
-    def load(v):
-        return pltpu.make_async_copy(state_hbm.at[v], state.at[v], load_sem.at[v])
-
-    for v in range(count):
-        load(v).start()
+    def load(first, size):
+        part = pl.ds(first, size)
+        return pltpu.make_async_copy(
+            state_hbm.at[part], state.at[part], load_sem.at[min(first, 1)]
+        )
+
+    load(0, 1).start()
+    load(1, count - 1).start()
 
     def reachable(dx):
         if dx == 0:
@@ -262,10 +265,9 @@
         guarded(reachable(dx), greet)
 
     def eps_copy(dx, dy):
-        slot = 3 * (dx + 1) + dy + 1
         return pltpu.make_async_remote_copy(
             src_ref=eps_out, dst_ref=around.at[1 - dx, 1 - dy],
-            send_sem=eps_send.at[slot], recv_sem=eps_recv.at[8 - slot],
+            send_sem=eps_sem.at[0], recv_sem=eps_sem.at[1],
             device_id=partner(dx, dy), device_id_type=mesh_id,
         )
 
@@ -276,31 +278,48 @@
             return ref.at[v, :, chords - 1 if last else 0]
         return ref.at[v, :, :, spans - 1 if last else 0]
 
-    def message(stage, k, v):
-        dx, dy = ways[k]
-        axis, up = k // 2, k % 2 == 0
-        return pltpu.make_async_remote_copy(
-            src_ref=side(faces[stage][axis], axis, v, up),
-            dst_ref=side(ghosts[stage][axis], axis, v, not up),
-            send_sem=send_sem.at[stage, k, v], recv_sem=recv_sem.at[stage, k, v],
-            device_id=partner(dx, dy), device_id_type=mesh_id,
-        )
+    def recv_sem(stage, axis, v):
+        if stage == 0:
+            return state_sem.at[axis, v]
+        return chord_sem if axis == 0 else flux_sem.at[v]
 
     def launch(stage, axis, v):
         for k in (2 * axis, 2 * axis + 1):
-            guarded(reachable(ways[k][0]), lambda k=k: message(stage, k, v).start())
-
-    def arrived(stage, axis, v):
-        for k in (2 * axis, 2 * axis + 1):
-            guarded(reachable(-ways[k][0]), lambda k=k: message(stage, k, v).wait_recv())
-
-    def sent(stage, axis, v):
-        for k in (2 * axis, 2 * axis + 1):
-            guarded(reachable(ways[k][0]), lambda k=k: message(stage, k, v).wait_send())
+            dx, dy = ways[k]
+            up = k % 2 == 0
+
+            def start():
+                pltpu.make_async_remote_copy(
+                    src_ref=side(faces[stage][axis], axis, v, up),
+                    dst_ref=side(ghosts[stage][axis], axis, v, not up),
+                    send_sem=send_sem.at[stage, axis], recv_sem=recv_sem(stage, axis, v),
+                    device_id=partner(dx, dy), device_id_type=mesh_id,
+                ).start()
+
+            guarded(reachable(dx), start)
+
+    two_sided = (me_c > 0) & (me_c + 1 < chord_size)
+
+    def await_bytes(ref, sem):
+        pltpu.make_async_copy(ref, ref, sem).wait()
+
+    def await_chord(ref, part, sem):
+        pl.when(two_sided)(lambda: await_bytes(ref.at[part, :, pl.ds(0, 2)], sem))
+        pl.when(jnp.logical_not(two_sided))(lambda: await_bytes(ref.at[part, :, pl.ds(0, 1)], sem))
+
+    def await_eps(sem):
+        pl.when(two_sided)(lambda: await_bytes(work.at[pl.ds(0, 8)], sem))
+        pl.when(jnp.logical_not(two_sided))(lambda: await_bytes(work.at[pl.ds(0, 5)], sem))
+
+    every = pl.ds(0, count)
+
+    def all_sent(stage):
+        await_chord(faces[stage][0], every, send_sem.at[stage, 0])
+        await_bytes(faces[stage][1].at[:, :, :, pl.ds(0, 2)], send_sem.at[stage, 1])
 
     masks = [row_masks(axis, chords, spans, lanes) for axis in range(2)]
 
-    def send_traces(axis, v):
+    def form_traces(axis, v):
         low = masks[axis][0]
         ends = [jnp.where(low, float(LEFT[i]), float(RIGHT[i])) for i in range(5)]
         out = whole(faces[0][axis])
@@ -308,27 +327,35 @@
             for j in range(5):
                 pts = points(axis, q, j)
                 out[v, 5 * q + j] = total_of([e * state[v, p] for e, p in zip(ends, pts)])
-        launch(0, axis, v)
-
-    load(0).wait()
-    sides = jnp.where(me_c > 0, 1, 0) + jnp.where(me_c + 1 < chord_size, 1, 0)
-    pl.semaphore_wait(barrier, 2 + 3 * sides)
-    send_traces(1, 0)
-    eps = sensor(lambda p: state[0, p], work)
-    eps_out[...] = eps
-    around[1, 1] = eps
+
+    with jax.named_scope("load0"):
+        load(0, 1).wait()
+    with jax.named_scope("sensor"):
+        form_traces(1, 0)
+        eps = sensor(lambda p: state[0, p], work)
+        eps_out[...] = eps
+        around[1, 1] = eps
+    with jax.named_scope("barrier"):
+        pl.semaphore_wait(barrier, 2 + 3 * jnp.where(two_sided, 2, 1))
     for dx, dy in offsets:
         guarded(reachable(dx), lambda dx=dx, dy=dy: eps_copy(dx, dy).start())
-
-    send_traces(0, 0)
-
-    def later_traces(v, carry):
-        load(v).wait()
-        for axis in (1, 0):
-            send_traces(axis, v)
-        return carry
-
-    lax.fori_loop(1, count, later_traces, 0)
+    launch(0, 1, 0)
+    with jax.named_scope("later"):
+        load(1, count - 1).wait()
+
+        def span_traces(v, carry):
+            form_traces(1, v)
+            launch(0, 1, v)
+            return carry
+
+        lax.fori_loop(1, count, span_traces, 0)
+
+        def chord_traces(v, carry):
+            form_traces(0, v)
+            launch(0, 0, v)
+            return carry
+
+        lax.fori_loop(0, count, chord_traces, 0)
 
     lane = lax.broadcasted_iota(jnp.int32, (rows, lanes), 1)
     first, last = lane == 0, lane == lanes - 1
@@ -345,11 +372,12 @@
                     grad[v, p] = value
         return carry
 
-    lax.fori_loop(0, count, normal_gradient, 0)
+    with jax.named_scope("ngrad"):
+        lax.fori_loop(0, count, normal_gradient, 0)
 
     row = lax.broadcasted_iota(jnp.int32, (rows, lanes), 0)
-    for dx, dy in offsets:
-        guarded(reachable(-dx), lambda dx=dx, dy=dy: eps_copy(dx, dy).wait_recv())
+    with jax.named_scope("epswait"):
+        await_eps(eps_sem.at[1])
 
     have_low = jnp.where(me_c > 0, spans, 0)
     have_high = jnp.where(me_c + 1 < chord_size, rows, rows - spans)
@@ -376,45 +404,40 @@
         neighbours[2].append(jnp.where(closed_high, 0.0, above))
     interpolate(neighbours, nu)
 
-    for axis in (1, 0):
+    shut = jnp.where(closed, -1.0, 0.0)
+
+    def across(axis, v):
         low, high = masks[axis]
         step = spans if axis == 0 else 1
-        shut = jnp.where(closed, -1.0, 0.0)
         mine, ghost = whole(faces[0][axis]), whole(ghosts[0][axis])
         out = whole(faces[1][axis])
-
-        def variable(v, carry):
-            arrived(0, axis, v)
-            for q in range(5):
-                for j in range(5):
-                    f = 5 * q + j
-                    pts = points(axis, q, j)
-                    parts = fold([state[v, p] for p in pts])
-                    left, right = traces(parts)
-                    beyond = ghost[v, f]
-                    if axis == 0:
-                        beyond = jnp.where(closed, mine[v, f], beyond)
-                    before = jnp.where(low, beyond, rolled(right, step, 0))
-                    after = jnp.where(high, beyond, rolled(left, -step, 0))
-                    gradient = slope(parts, before, after)
-                    parts = fold([nu[p] * g for p, g in zip(pts, gradient)])
-                    left, right = traces(parts)
-                    ends = jnp.where(low, left, right)
-                    out[v, f] = ends
-                    beyond = shut * ends if axis == 0 else 0.0
-                    before = jnp.where(low, beyond, rolled(right, step, 0))
-                    after = jnp.where(high, beyond, rolled(left, -step, 0))
-                    for p, value in zip(pts, slope(parts, before, after)):
-                        if axis == 1:
-                            acc[v, p] = value
-                        else:
-                            acc[v, p] += value
-            launch(1, axis, v)
-            return carry
-
-        lax.fori_loop(0, count, variable, 0)
-
-    def normal(v, carry):
+        for q in range(5):
+            for j in range(5):
+                f = 5 * q + j
+                pts = points(axis, q, j)
+                parts = fold([state[v, p] for p in pts])
+                left, right = traces(parts)
+                beyond = ghost[v, f]
+                if axis == 0:
+                    beyond = jnp.where(closed, mine[v, f], beyond)
+                before = jnp.where(low, beyond, rolled(right, step, 0))
+                after = jnp.where(high, beyond, rolled(left, -step, 0))
+                gradient = slope(parts, before, after)
+                parts = fold([nu[p] * g for p, g in zip(pts, gradient)])
+                left, right = traces(parts)
+                ends = jnp.where(low, left, right)
+                out[v, f] = ends
+                beyond = shut * ends if axis == 0 else 0.0
+                before = jnp.where(low, beyond, rolled(right, step, 0))
+                after = jnp.where(high, beyond, rolled(left, -step, 0))
+                for p, value in zip(pts, slope(parts, before, after)):
+                    if axis == 1:
+                        acc[v, p] = value
+                    else:
+                        acc[v, p] += value
+        launch(1, axis, v)
+
+    def normal(v):
         for q in range(5):
             for j in range(5):
                 pts = points(2, q, j)
@@ -424,14 +447,26 @@
                 after = jnp.where(last, -right, rolled(left, -1, 1))
                 for p, value in zip(pts, slope(parts, before, after)):
                     acc[v, p] += value
-        for axis in range(2):
-            sent(0, axis, v)
+
+    def variable(v, carry):
+        with jax.named_scope("wait_u1"):
+            await_bytes(ghosts[0][1].at[v, :, :, pl.ds(0, 2)], state_sem.at[1, v])
+        with jax.named_scope("span"):
+            across(1, v)
+        with jax.named_scope("wait_u0"):
+            await_chord(ghosts[0][0], v, state_sem.at[0, v])
+        with jax.named_scope("chord"):
+            across(0, v)
+        with jax.named_scope("normal"):
+            normal(v)
         return carry
 
-    lax.fori_loop(0, count, normal, 0)
-
-    for dx, dy in offsets:
-        guarded(reachable(dx), lambda dx=dx, dy=dy: eps_copy(dx, dy).wait_send())
+    with jax.named_scope("fluxes"):
+        lax.fori_loop(0, count, variable, 0)
+
+    with jax.named_scope("sent0"):
+        await_eps(eps_sem.at[0])
+        all_sent(0)
 
     lifts = [
         [
@@ -444,10 +479,8 @@
     edges[0] = edges[0] & jnp.logical_not(closed)
 
     def correct(v, carry):
-        for axis in range(2):
-            arrived(1, axis, v)
-        for axis in range(2):
-            sent(1, axis, v)
+        with jax.named_scope("wait_f1"):
+            await_bytes(ghosts[1][1].at[v, :, :, pl.ds(0, 2)], flux_sem.at[v])
         flux_c, flux_s = whole(ghosts[1][0]), whole(ghosts[1][1])
         for c in range(5):
             along = [
@@ -461,7 +494,12 @@
                     )
         return carry
 
-    lax.fori_loop(0, count, correct, 0)
+    with jax.named_scope("wait_f0"):
+        await_chord(ghosts[1][0], every, chord_sem)
+    with jax.named_scope("correct"):
+        lax.fori_loop(0, count, correct, 0)
+    with jax.named_scope("sent1"):
+        all_sent(1)
 
 
 def finish_kernel(acc, nu, residual_out, nu_out, sems):
@@ -504,11 +542,12 @@
             + [(count, 25, chords, spans, lanes)] * 8
         ]
         + [
+            pltpu.SemaphoreType.DMA((2,)),
+            pltpu.SemaphoreType.DMA((2,)),
+            pltpu.SemaphoreType.DMA((2, 2)),
+            pltpu.SemaphoreType.DMA((2, count)),
             pltpu.SemaphoreType.DMA((count,)),
-            pltpu.SemaphoreType.DMA((9,)),
-            pltpu.SemaphoreType.DMA((9,)),
-            pltpu.SemaphoreType.DMA((2, 4, count)),
-            pltpu.SemaphoreType.DMA((2, 4, count)),
+            pltpu.SemaphoreType.DMA,
         ],
         compiler_params=pltpu.CompilerParams(
             collective_id=0, has_side_effects=True, vmem_limit_bytes=VMEM_BYTES

time: 21.3 us -> 19.8 us (0.930)
  Pallas kernels: 20.6 us -> 19.1 us
    pallas_call x1, Pallas kernels: 18.9 us -> 17.4 us  [shards(): pl.pallas_call(functools.partial(local_kernel, sizes, count, chords, span...]
where the time goes in v3:
time: 19.8 us; the launch traced here: 19.7 us
  Pallas kernels  19.1 us (96%)
  between operations  0.64 us (3%)
    pallas_call x1, Pallas kernels, shards(): pl.pallas_call(functools.partial(local_kernel, sizes, count, chords, span...  17.4 us
    pallas_call x1, Pallas kernels, shards(): pl.pallas_call(finish_kernel, in_specs=[vmem, vmem], out_specs=[hbm, hbm]...  1.68 us

profile of v3, /device:TPU:0, one launch (start us, length us, event | category | flops | bytes accessed | tf_op | source)
XLA Modules:
  0.0 19.7 jit_solution(3681473576978966546)
XLA Ops:
  0.6 17.4 %shard_map.30 = (f32[125,8,128]{2,1,0:T(8,128)S(1)}, f32[5,125,8,128]{3,2,1,0:T(8,128)S(1)}) custom-call(f32[5,125,8,128]{3,2,1,0:T(8,128)} %bitcast.3), custom_call_target="tpu_custom_call" | custom-call | tf_op jit(solution)/shard_map/pallas_call | solution.py:528
  18.0 1.7 %shard_map.31 = (f32[5,125,8,128]{3,2,1,0:T(8,128)}, f32[125,8,128]{2,1,0:T(8,128)}) custom-call(f32[5,125,8,128]{3,2,1,0:T(8,128)S(1)} %get-tuple-element.6.acc, f32[125,8,128]{2,1,0:T(8,128)S(1)} %get-tuple-element.7.nu), custom_call_target="tpu_custom_call" | custom-call | tf_op jit(solution)/shard_map/pallas_call | solution.py:557

commit v4 on v3

--- a/solution.py
+++ b/solution.py
@@ -223,7 +223,7 @@
     state, grad, around, work, eps_out = refs[3:8]
     faces = (refs[8:10], refs[10:12])
     ghosts = (refs[12:14], refs[14:16])
-    load_sem, eps_sem, send_sem, state_sem, flux_sem, chord_sem = refs[16:]
+    load_sem, eps_sem, send_sem, state_sem, flux_sem, chord_sem, answer = refs[16:]
     rows, lanes = nu.shape[1:]
     chord_size, span_size = sizes
     me_c, me_s = lax.axis_index("chord"), lax.axis_index("span")
@@ -255,43 +255,56 @@
     def partner(dx, dy):
         return (me_c + dx, lax.rem(me_s + dy + span_size, span_size))
 
-    offsets = [(dx, dy) for dx in (0, -1, 1) for dy in (-1, 0, 1) if (dx, dy) != (0, 0)]
+    level = ((0, -1), (0, 1))
+    lower, upper = (tuple((dx, dy) for dy in (0, -1, 1)) for dx in (-1, 1))
+
+    def greet(sem, offsets):
+        for dx, dy in offsets:
+            pl.semaphore_signal(sem, inc=1, device_id=partner(dx, dy), device_id_type=mesh_id)
+
     barrier = pltpu.get_barrier_semaphore()
-    for dx, dy in offsets:
-
-        def greet(dx=dx, dy=dy):
-            pl.semaphore_signal(barrier, inc=1, device_id=partner(dx, dy), device_id_type=mesh_id)
-
-        guarded(reachable(dx), greet)
+    greet(barrier, level)
+    guarded(reachable(1), lambda: greet(barrier, upper))
 
     def eps_copy(dx, dy):
         return pltpu.make_async_remote_copy(
             src_ref=eps_out, dst_ref=around.at[1 - dx, 1 - dy],
-            send_sem=eps_sem.at[0], recv_sem=eps_sem.at[1],
+            send_sem=eps_sem.at[0], recv_sem=eps_sem.at[1 if dx == 0 else 2],
             device_id=partner(dx, dy), device_id_type=mesh_id,
         )
 
+    def column_copy():
+        return pltpu.make_async_remote_copy(
+            src_ref=around.at[1], dst_ref=around.at[0],
+            send_sem=eps_sem.at[0], recv_sem=eps_sem.at[2],
+            device_id=partner(1, 0), device_id_type=mesh_id,
+        )
+
     ways = ((1, 0), (-1, 0), (0, 1), (0, -1))
 
-    def side(ref, axis, v, last):
+    def side(ref, axis, v, last, part):
         if axis == 0:
-            return ref.at[v, :, chords - 1 if last else 0]
-        return ref.at[v, :, :, spans - 1 if last else 0]
+            return ref.at[v, part, chords - 1 if last else 0]
+        return ref.at[v, part, :, spans - 1 if last else 0]
 
     def recv_sem(stage, axis, v):
         if stage == 0:
             return state_sem.at[axis, v]
         return chord_sem if axis == 0 else flux_sem.at[v]
 
-    def launch(stage, axis, v):
-        for k in (2 * axis, 2 * axis + 1):
+    def send_eps(offsets):
+        for dx, dy in offsets:
+            eps_copy(dx, dy).start()
+
+    def launch(stage, axis, v, sides=(0, 1), part=pl.ds(0, 25)):
+        for k in (2 * axis + i for i in sides):
             dx, dy = ways[k]
             up = k % 2 == 0
 
             def start():
                 pltpu.make_async_remote_copy(
-                    src_ref=side(faces[stage][axis], axis, v, up),
-                    dst_ref=side(ghosts[stage][axis], axis, v, not up),
+                    src_ref=side(faces[stage][axis], axis, v, up, part),
+                    dst_ref=side(ghosts[stage][axis], axis, v, not up, part),
                     send_sem=send_sem.at[stage, axis], recv_sem=recv_sem(stage, axis, v),
                     device_id=partner(dx, dy), device_id_type=mesh_id,
                 ).start()
@@ -307,9 +320,11 @@
         pl.when(two_sided)(lambda: await_bytes(ref.at[part, :, pl.ds(0, 2)], sem))
         pl.when(jnp.logical_not(two_sided))(lambda: await_bytes(ref.at[part, :, pl.ds(0, 1)], sem))
 
-    def await_eps(sem):
-        pl.when(two_sided)(lambda: await_bytes(work.at[pl.ds(0, 8)], sem))
-        pl.when(jnp.logical_not(two_sided))(lambda: await_bytes(work.at[pl.ds(0, 5)], sem))
+    def await_eps(sem, base):
+        pl.when(two_sided)(lambda: await_bytes(work.at[pl.ds(0, base + 6)], sem))
+        pl.when(jnp.logical_not(two_sided))(
+            lambda: await_bytes(work.at[pl.ds(0, base + 3)], sem)
+        )
 
     every = pl.ds(0, count)
 
@@ -319,27 +334,30 @@
 
     masks = [row_masks(axis, chords, spans, lanes) for axis in range(2)]
 
-    def form_traces(axis, v):
+    def form_traces(axis, v, lines=range(5)):
         low = masks[axis][0]
         ends = [jnp.where(low, float(LEFT[i]), float(RIGHT[i])) for i in range(5)]
         out = whole(faces[0][axis])
-        for q in range(5):
+        for q in lines:
             for j in range(5):
                 pts = points(axis, q, j)
                 out[v, 5 * q + j] = total_of([e * state[v, p] for e, p in zip(ends, pts)])
 
     with jax.named_scope("load0"):
         load(0, 1).wait()
+    form_traces(1, 0, range(2))
+    with jax.named_scope("barrier"):
+        pl.semaphore_wait(barrier, 2 + jnp.where(me_c > 0, 3, 0))
+    launch(0, 1, 0, part=pl.ds(0, 10))
+    guarded(reachable(-1), lambda: greet(answer, ((-1, 0),)))
     with jax.named_scope("sensor"):
-        form_traces(1, 0)
         eps = sensor(lambda p: state[0, p], work)
         eps_out[...] = eps
         around[1, 1] = eps
-    with jax.named_scope("barrier"):
-        pl.semaphore_wait(barrier, 2 + 3 * jnp.where(two_sided, 2, 1))
-    for dx, dy in offsets:
-        guarded(reachable(dx), lambda dx=dx, dy=dy: eps_copy(dx, dy).start())
-    launch(0, 1, 0)
+    send_eps(level)
+    guarded(reachable(-1), lambda: send_eps(lower))
+    form_traces(1, 0, range(2, 5))
+    launch(0, 1, 0, part=pl.ds(10, 15))
     with jax.named_scope("later"):
         load(1, count - 1).wait()
 
@@ -352,7 +370,7 @@
 
         def chord_traces(v, carry):
             form_traces(0, v)
-            launch(0, 0, v)
+            launch(0, 0, v, (1,))
             return carry
 
         lax.fori_loop(0, count, chord_traces, 0)
@@ -375,9 +393,24 @@
     with jax.named_scope("ngrad"):
         lax.fori_loop(0, count, normal_gradient, 0)
 
+    with jax.named_scope("level"):
+        await_bytes(work.at[pl.ds(0, 2)], eps_sem.at[1])
+    with jax.named_scope("answer"):
+
+        @pl.when(reachable(1))
+        def _():
+            pl.semaphore_wait(answer, 1)
+            column_copy().start()
+
+        def chord_up(v, carry):
+            launch(0, 0, v, (0,))
+            return carry
+
+        lax.fori_loop(0, count, chord_up, 0)
+
     row = lax.broadcasted_iota(jnp.int32, (rows, lanes), 0)
     with jax.named_scope("epswait"):
-        await_eps(eps_sem.at[1])
+        await_eps(eps_sem.at[2], 0)
 
     have_low = jnp.where(me_c > 0, spans, 0)
     have_high = jnp.where(me_c + 1 < chord_size, rows, rows - spans)
@@ -457,15 +490,20 @@
             await_chord(ghosts[0][0], v, state_sem.at[0, v])
         with jax.named_scope("chord"):
             across(0, v)
-        with jax.named_scope("normal"):
-            normal(v)
         return carry
 
     with jax.named_scope("fluxes"):
         lax.fori_loop(0, count, variable, 0)
 
+    def rest(v, carry):
+        normal(v)
+        return carry
+
+    with jax.named_scope("normal"):
+        lax.fori_loop(0, count, rest, 0)
+
     with jax.named_scope("sent0"):
-        await_eps(eps_sem.at[0])
+        await_eps(eps_sem.at[0], 2)
         all_sent(0)
 
     lifts = [
@@ -543,11 +581,12 @@
         ]
         + [
             pltpu.SemaphoreType.DMA((2,)),
-            pltpu.SemaphoreType.DMA((2,)),
+            pltpu.SemaphoreType.DMA((3,)),
             pltpu.SemaphoreType.DMA((2, 2)),
             pltpu.SemaphoreType.DMA((2, count)),
             pltpu.SemaphoreType.DMA((count,)),
             pltpu.SemaphoreType.DMA,
+            pltpu.SemaphoreType.REGULAR,
         ],
         compiler_params=pltpu.CompilerParams(
             collective_id=0, has_side_effects=True, vmem_limit_bytes=VMEM_BYTES

time: 19.8 us -> 19.2 us (0.970)
  Pallas kernels: 19.1 us -> 18.4 us
    pallas_call x1, Pallas kernels: 17.4 us -> 16.7 us  [shards(): pl.pallas_call(functools.partial(local_kernel, sizes, count, chords, span...]
where the time goes in v4:
time: 19.2 us; the launch traced here: 19 us
  Pallas kernels  18.4 us (96%)
  between operations  0.64 us (3%)
    pallas_call x1, Pallas kernels, shards(): pl.pallas_call(functools.partial(local_kernel, sizes, count, chords, span...  16.7 us
    pallas_call x1, Pallas kernels, shards(): pl.pallas_call(finish_kernel, in_specs=[vmem, vmem], out_specs=[hbm, hbm]...  1.68 us

profile of v4, /device:TPU:0, one launch (start us, length us, event | category | flops | bytes accessed | tf_op | source)
XLA Modules:
  0.0 19.0 jit_solution(11629978188365688782)
XLA Ops:
  0.6 16.7 %shard_map.30 = (f32[125,8,128]{2,1,0:T(8,128)S(1)}, f32[5,125,8,128]{3,2,1,0:T(8,128)S(1)}) custom-call(f32[5,125,8,128]{3,2,1,0:T(8,128)} %bitcast.3), custom_call_target="tpu_custom_call" | custom-call | tf_op jit(solution)/shard_map/pallas_call | solution.py:566
  17.3 1.7 %shard_map.31 = (f32[5,125,8,128]{3,2,1,0:T(8,128)}, f32[125,8,128]{2,1,0:T(8,128)}) custom-call(f32[5,125,8,128]{3,2,1,0:T(8,128)S(1)} %get-tuple-element.6.acc, f32[125,8,128]{2,1,0:T(8,128)S(1)} %get-tuple-element.7.nu), custom_call_target="tpu_custom_call" | custom-call | tf_op jit(solution)/shard_map/pallas_call | solution.py:596

commit v5 on v4

--- a/solution.py
+++ b/solution.py
@@ -11,6 +11,7 @@
 
 VMEM_BYTES = 52_500_000
 FINISH_BYTES = 8_000_000
+LAG = 3
 EPS_SCALE = 0.01
 SENSOR_CENTRE = -3.0
 SENSOR_WIDTH = 1.5
@@ -220,10 +221,11 @@
 def local_kernel(sizes, count, chords, spans, *refs):
     state_hbm = refs[0]
     nu, acc = refs[1:3]
-    state, grad, around, work, eps_out = refs[3:8]
-    faces = (refs[8:10], refs[10:12])
-    ghosts = (refs[12:14], refs[14:16])
-    load_sem, eps_sem, send_sem, state_sem, flux_sem, chord_sem, answer = refs[16:]
+    state, around, work, eps_out = refs[3:7]
+    grads = refs[7:10]
+    faces = (refs[10:12], refs[12:14])
+    ghosts = (refs[14:16], refs[16:18])
+    load_sem, eps_sem, send_sem, state_sem, flux_sem, chord_sem, answer = refs[18:]
     rows, lanes = nu.shape[1:]
     chord_size, span_size = sizes
     me_c, me_s = lax.axis_index("chord"), lax.axis_index("span")
@@ -232,14 +234,18 @@
     def whole(ref):
         return ref.reshape(count, 25, rows, lanes)
 
-    def load(first, size):
+    def load(v, k, first, size):
         part = pl.ds(first, size)
         return pltpu.make_async_copy(
-            state_hbm.at[part], state.at[part], load_sem.at[min(first, 1)]
+            state_hbm.at[v, part], state.at[v, part], load_sem.at[k]
         )
 
-    load(0, 1).start()
-    load(1, count - 1).start()
+    start, remainder = load(0, 0, 0, 50), load(0, 1, 50, 75)
+    others = pltpu.make_async_copy(
+        state_hbm.at[pl.ds(1, count - 1)], state.at[pl.ds(1, count - 1)], load_sem.at[2]
+    )
+    for copy in (start, remainder, others):
+        copy.start()
 
     def reachable(dx):
         if dx == 0:
@@ -296,7 +302,7 @@
         for dx, dy in offsets:
             eps_copy(dx, dy).start()
 
-    def launch(stage, axis, v, sides=(0, 1), part=pl.ds(0, 25)):
+    def launch(stage, axis, v, sides=(0, 1), part=pl.ds(0, 25), only=None):
         for k in (2 * axis + i for i in sides):
             dx, dy = ways[k]
             up = k % 2 == 0
@@ -309,7 +315,14 @@
                     device_id=partner(dx, dy), device_id_type=mesh_id,
                 ).start()
 
-            guarded(reachable(dx), start)
+            allowed = reachable(dx) if only is None else only(partner(dx, dy)[1])
+            guarded(allowed, start)
+
+    def first_half(s):
+        return s < span_size // 2
+
+    def second_half(s):
+        return s >= span_size // 2
 
     two_sided = (me_c > 0) & (me_c + 1 < chord_size)
 
@@ -344,13 +357,14 @@
                 out[v, 5 * q + j] = total_of([e * state[v, p] for e, p in zip(ends, pts)])
 
     with jax.named_scope("load0"):
-        load(0, 1).wait()
+        start.wait()
     form_traces(1, 0, range(2))
     with jax.named_scope("barrier"):
         pl.semaphore_wait(barrier, 2 + jnp.where(me_c > 0, 3, 0))
     launch(0, 1, 0, part=pl.ds(0, 10))
     guarded(reachable(-1), lambda: greet(answer, ((-1, 0),)))
     with jax.named_scope("sensor"):
+        remainder.wait()
         eps = sensor(lambda p: state[0, p], work)
         eps_out[...] = eps
         around[1, 1] = eps
@@ -359,7 +373,7 @@
     form_traces(1, 0, range(2, 5))
     launch(0, 1, 0, part=pl.ds(10, 15))
     with jax.named_scope("later"):
-        load(1, count - 1).wait()
+        others.wait()
 
         def span_traces(v, carry):
             form_traces(1, v)
@@ -377,8 +391,18 @@
 
     lane = lax.broadcasted_iota(jnp.int32, (rows, lanes), 1)
     first, last = lane == 0, lane == lanes - 1
+    row = lax.broadcasted_iota(jnp.int32, (rows, lanes), 0)
+    have_low = jnp.where(me_c > 0, spans, 0)
+    have_high = jnp.where(me_c + 1 < chord_size, rows, rows - spans)
+    low_s, high_s = masks[1]
+    low_c, high_c = masks[0]
+    closed_low = row < spans - have_low
+    closed_high = row >= have_high
+    closed = closed_low | closed_high
+    shut = jnp.where(closed, 1.0, 0.0)
 
     def normal_gradient(v, carry):
+        grad = grads[2]
         for q in range(5):
             for j in range(5):
                 pts = points(2, q, j)
@@ -390,8 +414,30 @@
                     grad[v, p] = value
         return carry
 
+    def across_gradient(axis):
+        low, high = masks[axis]
+        step = spans if axis == 0 else 1
+        mine, grad = whole(faces[0][axis]), grads[axis]
+
+        def body(v, carry):
+            for q in range(5):
+                for j in range(5):
+                    pts = points(axis, q, j)
+                    parts = fold([state[v, p] for p in pts])
+                    left, right = traces(parts)
+                    beyond = shut * mine[v, 5 * q + j] if axis == 0 else 0.0
+                    before = jnp.where(low, beyond, rolled(right, step, 0))
+                    after = jnp.where(high, beyond, rolled(left, -step, 0))
+                    for p, value in zip(pts, slope(parts, before, after)):
+                        grad[v, p] = value
+            return carry
+
+        return body
+
     with jax.named_scope("ngrad"):
         lax.fori_loop(0, count, normal_gradient, 0)
+    with jax.named_scope("sgrad"):
+        lax.fori_loop(0, count, across_gradient(1), 0)
 
     with jax.named_scope("level"):
         await_bytes(work.at[pl.ds(0, 2)], eps_sem.at[1])
@@ -408,17 +454,12 @@
 
         lax.fori_loop(0, count, chord_up, 0)
 
-    row = lax.broadcasted_iota(jnp.int32, (rows, lanes), 0)
+    with jax.named_scope("cgrad"):
+        lax.fori_loop(0, count, across_gradient(0), 0)
+
     with jax.named_scope("epswait"):
         await_eps(eps_sem.at[2], 0)
 
-    have_low = jnp.where(me_c > 0, spans, 0)
-    have_high = jnp.where(me_c + 1 < chord_size, rows, rows - spans)
-    low_s, high_s = masks[1]
-    low_c, high_c = masks[0]
-    closed_low = row < spans - have_low
-    closed_high = row >= have_high
-    closed = closed_low | closed_high
     column = []
     for x in range(3):
         mine, left, right = around[x, 1], around[x, 0], around[x, 2]
@@ -437,75 +478,6 @@
         neighbours[2].append(jnp.where(closed_high, 0.0, above))
     interpolate(neighbours, nu)
 
-    shut = jnp.where(closed, -1.0, 0.0)
-
-    def across(axis, v):
-        low, high = masks[axis]
-        step = spans if axis == 0 else 1
-        mine, ghost = whole(faces[0][axis]), whole(ghosts[0][axis])
-        out = whole(faces[1][axis])
-        for q in range(5):
-            for j in range(5):
-                f = 5 * q + j
-                pts = points(axis, q, j)
-                parts = fold([state[v, p] for p in pts])
-                left, right = traces(parts)
-                beyond = ghost[v, f]
-                if axis == 0:
-                    beyond = jnp.where(closed, mine[v, f], beyond)
-                before = jnp.where(low, beyond, rolled(right, step, 0))
-                after = jnp.where(high, beyond, rolled(left, -step, 0))
-                gradient = slope(parts, before, after)
-                parts = fold([nu[p] * g for p, g in zip(pts, gradient)])
-                left, right = traces(parts)
-                ends = jnp.where(low, left, right)
-                out[v, f] = ends
-                beyond = shut * ends if axis == 0 else 0.0
-                before = jnp.where(low, beyond, rolled(right, step, 0))
-                after = jnp.where(high, beyond, rolled(left, -step, 0))
-                for p, value in zip(pts, slope(parts, before, after)):
-                    if axis == 1:
-                        acc[v, p] = value
-                    else:
-                        acc[v, p] += value
-        launch(1, axis, v)
-
-    def normal(v):
-        for q in range(5):
-            for j in range(5):
-                pts = points(2, q, j)
-                parts = fold([nu[p] * grad[v, p] for p in pts])
-                left, right = traces(parts)
-                before = jnp.where(first, -left, rolled(right, 1, 1))
-                after = jnp.where(last, -right, rolled(left, -1, 1))
-                for p, value in zip(pts, slope(parts, before, after)):
-                    acc[v, p] += value
-
-    def variable(v, carry):
-        with jax.named_scope("wait_u1"):
-            await_bytes(ghosts[0][1].at[v, :, :, pl.ds(0, 2)], state_sem.at[1, v])
-        with jax.named_scope("span"):
-            across(1, v)
-        with jax.named_scope("wait_u0"):
-            await_chord(ghosts[0][0], v, state_sem.at[0, v])
-        with jax.named_scope("chord"):
-            across(0, v)
-        return carry
-
-    with jax.named_scope("fluxes"):
-        lax.fori_loop(0, count, variable, 0)
-
-    def rest(v, carry):
-        normal(v)
-        return carry
-
-    with jax.named_scope("normal"):
-        lax.fori_loop(0, count, rest, 0)
-
-    with jax.named_scope("sent0"):
-        await_eps(eps_sem.at[0], 2)
-        all_sent(0)
-
     lifts = [
         [
             jnp.where(low, float(HALF_LEFT[i]), jnp.where(high, float(HALF_RIGHT[i]), 0.0))
@@ -515,6 +487,82 @@
     ]
     edges = [(low | high) for low, high in masks]
     edges[0] = edges[0] & jnp.logical_not(closed)
+    full_edge = (chords == 1, spans <= 2)
+
+    def outside(ref, axis, v, f):
+        value = ref[v, f]
+        return value if full_edge[axis] else jnp.where(edges[axis], value, 0.0)
+
+    def across(axis, v):
+        low, high = masks[axis]
+        step = spans if axis == 0 else 1
+        grad, ghost, out = grads[axis], whole(ghosts[0][axis]), whole(faces[1][axis])
+        for q in range(5):
+            for j in range(5):
+                f = 5 * q + j
+                pts = points(axis, q, j)
+                beyond = outside(ghost, axis, v, f)
+                gradient = [grad[v, p] + lift * beyond for p, lift in zip(pts, lifts[axis])]
+                parts = fold([nu[p] * g for p, g in zip(pts, gradient)])
+                left, right = traces(parts)
+                ends = jnp.where(low, left, right)
+                out[v, f] = ends
+                beyond = -shut * ends if axis == 0 else 0.0
+                before = jnp.where(low, beyond, rolled(right, step, 0))
+                after = jnp.where(high, beyond, rolled(left, -step, 0))
+                for p, value in zip(pts, slope(parts, before, after)):
+                    if axis == 1:
+                        acc[v, p] = value
+                    else:
+                        acc[v, p] += value
+
+    def normal(v):
+        for q in range(5):
+            for j in range(5):
+                pts = points(2, q, j)
+                parts = fold([nu[p] * grads[2][v, p] for p in pts])
+                left, right = traces(parts)
+                before = jnp.where(first, -left, rolled(right, 1, 1))
+                after = jnp.where(last, -right, rolled(left, -1, 1))
+                for p, value in zip(pts, slope(parts, before, after)):
+                    acc[v, p] += value
+
+    lag = min(LAG, count)
+
+    def variable(v, carry):
+        with jax.named_scope("wait_u1"):
+            await_bytes(ghosts[0][1].at[v, :, :, pl.ds(0, 2)], state_sem.at[1, v])
+        with jax.named_scope("span"):
+            across(1, v)
+            launch(1, 1, v, only=first_half)
+        with jax.named_scope("wait_u0"):
+            await_chord(ghosts[0][0], v, state_sem.at[0, v])
+        with jax.named_scope("chord"):
+            across(0, v)
+            launch(1, 0, v)
+            due = v >= lag
+            launch(1, 1, jnp.maximum(v - lag, 0), only=lambda s: second_half(s) & due)
+        return carry
+
+    with jax.named_scope("fluxes"):
+        lax.fori_loop(0, count, variable, 0)
+
+    def launch_rest(v, carry):
+        launch(1, 1, v, only=second_half)
+        return carry
+
+    lax.fori_loop(count - lag, count, launch_rest, 0)
+
+    def rest(v, carry):
+        normal(v)
+        return carry
+
+    with jax.named_scope("normal"):
+        lax.fori_loop(0, count, rest, 0)
+
+    with jax.named_scope("sent0"):
+        await_eps(eps_sem.at[0], 2)
+        all_sent(0)
 
     def correct(v, carry):
         with jax.named_scope("wait_f1"):
@@ -522,8 +570,8 @@
         flux_c, flux_s = whole(ghosts[1][0]), whole(ghosts[1][1])
         for c in range(5):
             along = [
-                [jnp.where(edges[0], flux_c[v, 5 * b + c], 0.0) for b in range(5)],
-                [jnp.where(edges[1], flux_s[v, 5 * a + c], 0.0) for a in range(5)],
+                [outside(flux_c, 0, v, 5 * b + c) for b in range(5)],
+                [outside(flux_s, 1, v, 5 * a + c) for a in range(5)],
             ]
             for a in range(5):
                 for b in range(5):
@@ -572,15 +620,17 @@
             pltpu.VMEM(shape, f32)
             for shape in [
                 (count, npts, rows, lanes),
-                (count, npts, rows, lanes),
                 (3, 3, rows, lanes),
                 (npts, rows, lanes),
                 (rows, lanes),
+                (count, npts, rows, lanes),
+                (count, npts, rows, lanes),
+                (count, npts, rows, lanes),
             ]
             + [(count, 25, chords, spans, lanes)] * 8
         ]
         + [
-            pltpu.SemaphoreType.DMA((2,)),
+            pltpu.SemaphoreType.DMA((3,)),
             pltpu.SemaphoreType.DMA((3,)),
             pltpu.SemaphoreType.DMA((2, 2)),
             pltpu.SemaphoreType.DMA((2, count)),

time: 19.2 us -> 18.2 us (0.948)
  Pallas kernels: 18.4 us -> 17.4 us
    pallas_call x1, Pallas kernels: 16.7 us -> 15.7 us  [shards(): pl.pallas_call(functools.partial(local_kernel, sizes, count, chords, span...]
where the time goes in v5:
time: 18.2 us; the launch traced here: 18 us
  Pallas kernels  17.4 us (96%)
  between operations  0.64 us (4%)
    pallas_call x1, Pallas kernels, shards(): pl.pallas_call(functools.partial(local_kernel, sizes, count, chords, span...  15.7 us
    pallas_call x1, Pallas kernels, shards(): pl.pallas_call(finish_kernel, in_specs=[vmem, vmem], out_specs=[hbm, hbm]...  1.68 us

profile of v5, /device:TPU:0, one launch (start us, length us, event | category | flops | bytes accessed | tf_op | source)
XLA Modules:
  0.0 18.0 jit_solution(2678781362703626170)
XLA Ops:
  0.6 15.7 %shard_map.30 = (f32[125,8,128]{2,1,0:T(8,128)S(1)}, f32[5,125,8,128]{3,2,1,0:T(8,128)S(1)}) custom-call(f32[5,125,8,128]{3,2,1,0:T(8,128)} %bitcast.3), custom_call_target="tpu_custom_call" | custom-call | tf_op jit(solution)/shard_map/pallas_call | solution.py:614
  16.3 1.7 %shard_map.31 = (f32[5,125,8,128]{3,2,1,0:T(8,128)}, f32[125,8,128]{2,1,0:T(8,128)}) custom-call(f32[5,125,8,128]{3,2,1,0:T(8,128)S(1)} %get-tuple-element.6.acc, f32[125,8,128]{2,1,0:T(8,128)S(1)} %get-tuple-element.7.nu), custom_call_target="tpu_custom_call" | custom-call | tf_op jit(solution)/shard_map/pallas_call | solution.py:646

commit v6 on v5

--- a/solution.py
+++ b/solution.py
@@ -119,46 +119,51 @@
     return [25 * q + 5 * j + i for i in range(5)]
 
 
-def modal_line(u):
-    s0, s1, mid, d0, d1 = fold(u)
-    out = []
-    for k in range(5):
-        m = [float(x) for x in MODAL[k]]
-        out.append(m[0] * s0 + m[1] * s1 + m[2] * mid if k % 2 == 0 else m[0] * d0 + m[1] * d1)
+TOP = [float(x) for x in MODAL[4]]
+WEIGHTS = [float(x) for x in GAUSS_WEIGHTS]
+
+
+def total_of(values):
+    out = values[0]
+    for value in values[1:]:
+        out = out + value
     return out
 
 
-def sensor(load, work):
-    def first(q, carry):
-        for j in range(5):
-            pts = points(0, q, j)
-            for i, value in zip(pts, modal_line([load(p) for p in pts])):
-                work[i] = value
-        return carry
-
-    lax.fori_loop(0, 5, first, 0)
-
-    def second(q, carry):
-        total, high = carry
-        plane = {}
-        for c in range(5):
-            for b, value in enumerate(modal_line([work[25 * q + 5 * b + c] for b in range(5)])):
-                plane[b, c] = value
-        low = jnp.zeros_like(total)
-        edge = jnp.zeros_like(total)
+def symmetric(coefficients, u):
+    c = coefficients
+    return c[0] * (u[0] + u[4]) + c[1] * (u[1] + u[3]) + c[2] * u[2]
+
+
+def energy(values):
+    return symmetric(WEIGHTS, [x * x for x in values])
+
+
+def sensor(load):
+    planes = {"y": [], "z": [], "yz": [], "total": [], "ez": [], "ey": [], "eyz": []}
+    top_x = {}
+    for a in range(5):
+        u = [[load(25 * a + 5 * b + c) for c in range(5)] for b in range(5)]
         for b in range(5):
-            line = modal_line([plane[b, c] for c in range(5)])
-            squares = [x * x for x in line]
-            if b < 4:
-                low = low + ((squares[0] + squares[1]) + (squares[2] + squares[3]))
-                edge = edge + squares[4]
-            else:
-                edge = edge + ((squares[0] + squares[1]) + (squares[2] + squares[3])) + squares[4]
-        plane_total = low + edge
-        return total + plane_total, high + jnp.where(q == 4, plane_total, edge)
-
-    zero = jnp.zeros(work.shape[1:], jnp.float32)
-    total, high = lax.fori_loop(0, 5, second, (zero, zero))
+            for c in range(5):
+                term = TOP[a] * u[b][c]
+                top_x[b, c] = term if a == 0 else top_x[b, c] + term
+        z = [symmetric(TOP, u[b]) for b in range(5)]
+        y = [symmetric(TOP, [u[b][c] for b in range(5)]) for c in range(5)]
+        yz = symmetric(TOP, z)
+        planes["total"].append(symmetric(WEIGHTS, [energy(u[b]) for b in range(5)]))
+        planes["ez"].append(energy(z))
+        planes["ey"].append(energy(y))
+        planes["eyz"].append(yz * yz)
+        planes["z"].append(z)
+        planes["y"].append(y)
+        planes["yz"].append(yz)
+    total, e_z, e_y, e_yz = (symmetric(WEIGHTS, planes[k]) for k in ("total", "ez", "ey", "eyz"))
+    x_z = [symmetric(TOP, [planes["z"][a][b] for a in range(5)]) for b in range(5)]
+    x_y = [symmetric(TOP, [planes["y"][a][c] for a in range(5)]) for c in range(5)]
+    x_yz = symmetric(TOP, planes["yz"])
+    e_x = symmetric(WEIGHTS, [energy([top_x[b, c] for c in range(5)]) for b in range(5)])
+    high = e_x + (e_y - energy(x_y)) + ((e_z - energy(x_z)) - (e_yz - x_yz * x_yz))
     level = jnp.log(jnp.maximum(high / (total + ENERGY_EPS), RATIO_FLOOR)) * (1.0 / math.log(10.0))
     ramp = jnp.clip((level - SENSOR_CENTRE) / SENSOR_WIDTH, -1.0, 1.0)
     return EPS_SCALE * 0.5 * (1.0 + jnp.sin(0.5 * math.pi * ramp))
@@ -211,13 +216,6 @@
     return place == 0, place == spans - 1
 
 
-def total_of(values):
-    out = values[0]
-    for value in values[1:]:
-        out = out + value
-    return out
-
-
 def local_kernel(sizes, count, chords, spans, *refs):
     state_hbm = refs[0]
     nu, acc = refs[1:3]
@@ -234,19 +232,6 @@
     def whole(ref):
         return ref.reshape(count, 25, rows, lanes)
 
-    def load(v, k, first, size):
-        part = pl.ds(first, size)
-        return pltpu.make_async_copy(
-            state_hbm.at[v, part], state.at[v, part], load_sem.at[k]
-        )
-
-    start, remainder = load(0, 0, 0, 50), load(0, 1, 50, 75)
-    others = pltpu.make_async_copy(
-        state_hbm.at[pl.ds(1, count - 1)], state.at[pl.ds(1, count - 1)], load_sem.at[2]
-    )
-    for copy in (start, remainder, others):
-        copy.start()
-
     def reachable(dx):
         if dx == 0:
             return None
@@ -270,6 +255,15 @@
 
     barrier = pltpu.get_barrier_semaphore()
     greet(barrier, level)
+
+    def load(k, *part):
+        return pltpu.make_async_copy(state_hbm.at[part], state.at[part], load_sem.at[k])
+
+    start, remainder = load(0, 0, pl.ds(0, 50)), load(1, 0, pl.ds(50, 75))
+    second, others = load(2, pl.ds(1, 1)), load(3, pl.ds(2, count - 2))
+    for copy in (start, remainder, second, others):
+        copy.start()
+
     guarded(reachable(1), lambda: greet(barrier, upper))
 
     def eps_copy(dx, dy):
@@ -365,7 +359,7 @@
     guarded(reachable(-1), lambda: greet(answer, ((-1, 0),)))
     with jax.named_scope("sensor"):
         remainder.wait()
-        eps = sensor(lambda p: state[0, p], work)
+        eps = sensor(lambda p: state[0, p])
         eps_out[...] = eps
         around[1, 1] = eps
     send_eps(level)
@@ -373,14 +367,15 @@
     form_traces(1, 0, range(2, 5))
     launch(0, 1, 0, part=pl.ds(10, 15))
     with jax.named_scope("later"):
-        others.wait()
-
         def span_traces(v, carry):
             form_traces(1, v)
             launch(0, 1, v)
             return carry
 
-        lax.fori_loop(1, count, span_traces, 0)
+        second.wait()
+        span_traces(1, 0)
+        others.wait()
+        lax.fori_loop(2, count, span_traces, 0)
 
         def chord_traces(v, carry):
             form_traces(0, v)
@@ -589,11 +584,10 @@
 
 
 def finish_kernel(acc, nu, residual_out, nu_out, sems):
-    copies = [
-        pltpu.make_async_copy(acc.at[v], residual_out.at[v], sems.at[v])
-        for v in range(acc.shape[0])
-    ]
-    copies.append(pltpu.make_async_copy(nu, nu_out, sems.at[acc.shape[0]]))
+    copies = (
+        pltpu.make_async_copy(acc, residual_out, sems.at[0]),
+        pltpu.make_async_copy(nu, nu_out, sems.at[1]),
+    )
     for copy in copies:
         copy.start()
     for copy in copies:
@@ -621,7 +615,7 @@
             for shape in [
                 (count, npts, rows, lanes),
                 (3, 3, rows, lanes),
-                (npts, rows, lanes),
+                (8, rows, lanes),
                 (rows, lanes),
                 (count, npts, rows, lanes),
                 (count, npts, rows, lanes),
@@ -630,7 +624,7 @@
             + [(count, 25, chords, spans, lanes)] * 8
         ]
         + [
-            pltpu.SemaphoreType.DMA((3,)),
+            pltpu.SemaphoreType.DMA((4,)),
             pltpu.SemaphoreType.DMA((3,)),
             pltpu.SemaphoreType.DMA((2, 2)),
             pltpu.SemaphoreType.DMA((2, count)),
@@ -648,7 +642,7 @@
         in_specs=[vmem, vmem],
         out_specs=[hbm, hbm],
         out_shape=[full(count, npts, rows, lanes), full(npts, rows, lanes)],
-        scratch_shapes=[pltpu.SemaphoreType.DMA((count + 1,))],
+        scratch_shapes=[pltpu.SemaphoreType.DMA((2,))],
         compiler_params=pltpu.CompilerParams(vmem_limit_bytes=FINISH_BYTES),
     )(residual, nu)
     return residual.reshape(state.shape), nu.reshape(npts, chords, spans, lanes)

time: 18.2 us -> 18.1 us (level)
  no operation moved by 1% of the time
where the time goes in v6:
time: 18.1 us; the launch traced here: 17.9 us
  Pallas kernels  17.3 us (96%)
  between operations  0.64 us (4%)
    pallas_call x1, Pallas kernels, shards(): pl.pallas_call(functools.partial(local_kernel, sizes, count, chords, span...  15.6 us
    pallas_call x1, Pallas kernels, shards(): pl.pallas_call(finish_kernel, in_specs=[vmem, vmem], out_specs=[hbm, hbm]...  1.65 us

profile of v6, /device:TPU:0, one launch (start us, length us, event | category | flops | bytes accessed | tf_op | source)
XLA Modules:
  0.0 17.9 jit_solution(12583247832314703124)
XLA Ops:
  0.6 15.6 %shard_map.30 = (f32[125,8,128]{2,1,0:T(8,128)S(1)}, f32[5,125,8,128]{3,2,1,0:T(8,128)S(1)}) custom-call(f32[5,125,8,128]{3,2,1,0:T(8,128)} %bitcast.3), custom_call_target="tpu_custom_call" | custom-call | tf_op jit(solution)/shard_map/pallas_call | solution.py:608
  16.3 1.6 %shard_map.31 = (f32[5,125,8,128]{3,2,1,0:T(8,128)}, f32[125,8,128]{2,1,0:T(8,128)}) custom-call(f32[5,125,8,128]{3,2,1,0:T(8,128)S(1)} %get-tuple-element.6.acc, f32[125,8,128]{2,1,0:T(8,128)S(1)} %get-tuple-element.7.nu), custom_call_target="tpu_custom_call" | custom-call | tf_op jit(solution)/shard_map/pallas_call | solution.py:640

commit v7 on v6

--- a/solution.py
+++ b/solution.py
@@ -219,11 +219,11 @@
 def local_kernel(sizes, count, chords, spans, *refs):
     state_hbm = refs[0]
     nu, acc = refs[1:3]
-    state, around, work, eps_out = refs[3:7]
-    grads = refs[7:10]
-    faces = (refs[10:12], refs[12:14])
-    ghosts = (refs[14:16], refs[16:18])
-    load_sem, eps_sem, send_sem, state_sem, flux_sem, chord_sem, answer = refs[18:]
+    state, around, tally = refs[3:6]
+    grads = refs[6:9]
+    faces = (refs[9:11], refs[11:13])
+    ghosts = (refs[13:15], refs[15:17])
+    load_sem, eps_sem, send_sem, state_sem, flux_sem, chord_sem, answer = refs[17:]
     rows, lanes = nu.shape[1:]
     chord_size, span_size = sizes
     me_c, me_s = lax.axis_index("chord"), lax.axis_index("span")
@@ -231,6 +231,8 @@
 
     def whole(ref):
         return ref.reshape(count, 25, rows, lanes)
+
+    all_eps = around.reshape(3, 3, rows, lanes)
 
     def reachable(dx):
         if dx == 0:
@@ -259,23 +261,27 @@
     def load(k, *part):
         return pltpu.make_async_copy(state_hbm.at[part], state.at[part], load_sem.at[k])
 
-    start, remainder = load(0, 0, pl.ds(0, 50)), load(1, 0, pl.ds(50, 75))
+    start, remainder = load(0, 0, pl.ds(0, 75)), load(1, 0, pl.ds(75, 50))
     second, others = load(2, pl.ds(1, 1)), load(3, pl.ds(2, count - 2))
     for copy in (start, remainder, second, others):
         copy.start()
 
     guarded(reachable(1), lambda: greet(barrier, upper))
 
+    def edge_of(step, size):
+        return pl.ds(0, size) if step == 0 else (size - 1 if step == 1 else 0)
+
     def eps_copy(dx, dy):
+        part = (edge_of(dx, chords), edge_of(dy, spans))
         return pltpu.make_async_remote_copy(
-            src_ref=eps_out, dst_ref=around.at[1 - dx, 1 - dy],
+            src_ref=around.at[(1, 1) + part], dst_ref=around.at[(1 - dx, 1 - dy) + part],
             send_sem=eps_sem.at[0], recv_sem=eps_sem.at[1 if dx == 0 else 2],
             device_id=partner(dx, dy), device_id_type=mesh_id,
         )
 
     def column_copy():
         return pltpu.make_async_remote_copy(
-            src_ref=around.at[1], dst_ref=around.at[0],
+            src_ref=around.at[1, :, chords - 1], dst_ref=around.at[0, :, chords - 1],
             send_sem=eps_sem.at[0], recv_sem=eps_sem.at[2],
             device_id=partner(1, 0), device_id_type=mesh_id,
         )
@@ -327,11 +333,14 @@
         pl.when(two_sided)(lambda: await_bytes(ref.at[part, :, pl.ds(0, 2)], sem))
         pl.when(jnp.logical_not(two_sided))(lambda: await_bytes(ref.at[part, :, pl.ds(0, 1)], sem))
 
-    def await_eps(sem, base):
-        pl.when(two_sided)(lambda: await_bytes(work.at[pl.ds(0, base + 6)], sem))
-        pl.when(jnp.logical_not(two_sided))(
-            lambda: await_bytes(work.at[pl.ds(0, base + 3)], sem)
-        )
+    def await_eps(sem, base, below, above):
+        has_below, has_above = me_c > 0, me_c + 1 < chord_size
+        for use_below in (False, True):
+            for use_above in (False, True):
+                size = base + use_below * below + use_above * above
+                if size:
+                    case = (has_below == use_below) & (has_above == use_above)
+                    pl.when(case)(lambda size=size: await_bytes(tally.at[pl.ds(0, size)], sem))
 
     every = pl.ds(0, count)
 
@@ -352,20 +361,19 @@
 
     with jax.named_scope("load0"):
         start.wait()
-    form_traces(1, 0, range(2))
+    form_traces(1, 0, range(3))
     with jax.named_scope("barrier"):
         pl.semaphore_wait(barrier, 2 + jnp.where(me_c > 0, 3, 0))
-    launch(0, 1, 0, part=pl.ds(0, 10))
+    launch(0, 1, 0, part=pl.ds(0, 15))
     guarded(reachable(-1), lambda: greet(answer, ((-1, 0),)))
     with jax.named_scope("sensor"):
         remainder.wait()
         eps = sensor(lambda p: state[0, p])
-        eps_out[...] = eps
-        around[1, 1] = eps
+        all_eps[1, 1] = eps
     send_eps(level)
     guarded(reachable(-1), lambda: send_eps(lower))
-    form_traces(1, 0, range(2, 5))
-    launch(0, 1, 0, part=pl.ds(10, 15))
+    form_traces(1, 0, range(3, 5))
+    launch(0, 1, 0, part=pl.ds(15, 10))
     with jax.named_scope("later"):
         def span_traces(v, carry):
             form_traces(1, v)
@@ -435,7 +443,7 @@
         lax.fori_loop(0, count, across_gradient(1), 0)
 
     with jax.named_scope("level"):
-        await_bytes(work.at[pl.ds(0, 2)], eps_sem.at[1])
+        await_bytes(tally.at[pl.ds(0, 2 * chords)], eps_sem.at[1])
     with jax.named_scope("answer"):
 
         @pl.when(reachable(1))
@@ -453,11 +461,11 @@
         lax.fori_loop(0, count, across_gradient(0), 0)
 
     with jax.named_scope("epswait"):
-        await_eps(eps_sem.at[2], 0)
+        await_eps(eps_sem.at[2], 0, 3 * spans, spans + 2)
 
     column = []
     for x in range(3):
-        mine, left, right = around[x, 1], around[x, 0], around[x, 2]
+        mine, left, right = all_eps[x, 1], all_eps[x, 0], all_eps[x, 2]
         column.append([
             jnp.where(low_s, rolled(left, 1 - spans, 0), rolled(mine, 1, 0)),
             mine,
@@ -556,7 +564,7 @@
         lax.fori_loop(0, count, rest, 0)
 
     with jax.named_scope("sent0"):
-        await_eps(eps_sem.at[0], 2)
+        await_eps(eps_sem.at[0], 2 * chords, spans + 2, 3 * spans)
         all_sent(0)
 
     def correct(v, carry):
@@ -614,9 +622,8 @@
             pltpu.VMEM(shape, f32)
             for shape in [
                 (count, npts, rows, lanes),
-                (3, 3, rows, lanes),
-                (8, rows, lanes),
-                (rows, lanes),
+                (3, 3, chords, spans, lanes),
+                (2 * chords + 4 * spans + 2, 1, lanes),
                 (count, npts, rows, lanes),
                 (count, npts, rows, lanes),
                 (count, npts, rows, lanes),

time: 18.1 us -> 17.9 us (0.989)
  Pallas kernels: 17.3 us -> 17.1 us
where the time goes in v7:
time: 17.9 us; the launch traced here: 17.8 us
  Pallas kernels  17.1 us (96%)
  between operations  0.64 us (4%)
    pallas_call x1, Pallas kernels, shards(): pl.pallas_call(functools.partial(local_kernel, sizes, count, chords, span...  15.5 us
    pallas_call x1, Pallas kernels, shards(): pl.pallas_call(finish_kernel, in_specs=[vmem, vmem], out_specs=[hbm, hbm]...  1.65 us

profile of v7, /device:TPU:0, one launch (start us, length us, event | category | flops | bytes accessed | tf_op | source)
XLA Modules:
  0.0 17.8 jit_solution(3317520658637923458)
XLA Ops:
  0.6 15.5 %shard_map.30 = (f32[125,8,128]{2,1,0:T(8,128)S(1)}, f32[5,125,8,128]{3,2,1,0:T(8,128)S(1)}) custom-call(f32[5,125,8,128]{3,2,1,0:T(8,128)} %bitcast.3), custom_call_target="tpu_custom_call" | custom-call | tf_op jit(solution)/shard_map/pallas_call | solution.py:616
  16.1 1.6 %shard_map.31 = (f32[5,125,8,128]{3,2,1,0:T(8,128)}, f32[125,8,128]{2,1,0:T(8,128)}) custom-call(f32[5,125,8,128]{3,2,1,0:T(8,128)S(1)} %get-tuple-element.6.acc, f32[125,8,128]{2,1,0:T(8,128)S(1)} %get-tuple-element.7.nu), custom_call_target="tpu_custom_call" | custom-call | tf_op jit(solution)/shard_map/pallas_call | solution.py:647

commit v8 on v7

--- a/solution.py
+++ b/solution.py
@@ -9,8 +9,9 @@
 from jax.experimental.pallas import tpu as pltpu
 from jax.sharding import PartitionSpec as P
 
-VMEM_BYTES = 52_500_000
+VMEM_BYTES = 50_750_000
 FINISH_BYTES = 8_000_000
+HELD = 2
 LAG = 3
 EPS_SCALE = 0.01
 SENSOR_CENTRE = -3.0
@@ -216,13 +217,47 @@
     return place == 0, place == spans - 1
 
 
+def closed_rows(chord_size, chords, spans, lanes):
+    rows = chords * spans
+    me_c = lax.axis_index("chord")
+    row = lax.broadcasted_iota(jnp.int32, (rows, lanes), 0)
+    have_low = jnp.where(me_c > 0, spans, 0)
+    have_high = jnp.where(me_c + 1 < chord_size, rows, rows - spans)
+    return row < spans - have_low, row >= have_high
+
+
+def boundary_lifts(masks, closed):
+    lifts = [
+        [
+            jnp.where(low, float(HALF_LEFT[i]), jnp.where(high, float(HALF_RIGHT[i]), 0.0))
+            for i in range(5)
+        ]
+        for low, high in masks
+    ]
+    edges = [(low | high) for low, high in masks]
+    edges[0] = edges[0] & jnp.logical_not(closed)
+    return lifts, edges
+
+
+def masked_edge(value, axis, edges, spans):
+    return value if axis == 1 and spans <= 2 else jnp.where(edges[axis], value, 0.0)
+
+
+def add_fluxes(flux, lifts, store):
+    for c in range(5):
+        along = [[flux(axis, 5 * m + c) for m in range(5)] for axis in range(2)]
+        for a in range(5):
+            for b in range(5):
+                store(25 * a + 5 * b + c, lifts[0][a] * along[0][b] + lifts[1][b] * along[1][a])
+
+
 def local_kernel(sizes, count, chords, spans, *refs):
     state_hbm = refs[0]
     nu, acc = refs[1:3]
-    state, around, tally = refs[3:6]
-    grads = refs[6:9]
-    faces = (refs[9:11], refs[11:13])
-    ghosts = (refs[13:15], refs[15:17])
+    state, around, tally = refs[5:8]
+    grads = refs[8:11]
+    faces = (refs[11:13], refs[13:15])
+    ghosts = (refs[15:17], refs[3:5])
     load_sem, eps_sem, send_sem, state_sem, flux_sem, chord_sem, answer = refs[17:]
     rows, lanes = nu.shape[1:]
     chord_size, span_size = sizes
@@ -323,6 +358,9 @@
 
     def second_half(s):
         return s >= span_size // 2
+
+    def by_one_link(s):
+        return (s % 4 == 1) | (s % 4 == 2)
 
     two_sided = (me_c > 0) & (me_c + 1 < chord_size)
 
@@ -377,9 +415,11 @@
     with jax.named_scope("later"):
         def span_traces(v, carry):
             form_traces(1, v)
-            launch(0, 1, v)
+            early = v < count - held
+            launch(0, 1, v, only=lambda s: jnp.logical_not(by_one_link(s)) | early)
             return carry
 
+        held = min(HELD, count - 1)
         second.wait()
         span_traces(1, 0)
         others.wait()
@@ -394,13 +434,9 @@
 
     lane = lax.broadcasted_iota(jnp.int32, (rows, lanes), 1)
     first, last = lane == 0, lane == lanes - 1
-    row = lax.broadcasted_iota(jnp.int32, (rows, lanes), 0)
-    have_low = jnp.where(me_c > 0, spans, 0)
-    have_high = jnp.where(me_c + 1 < chord_size, rows, rows - spans)
     low_s, high_s = masks[1]
     low_c, high_c = masks[0]
-    closed_low = row < spans - have_low
-    closed_high = row >= have_high
+    closed_low, closed_high = closed_rows(sizes[0], chords, spans, lanes)
     closed = closed_low | closed_high
     shut = jnp.where(closed, 1.0, 0.0)
 
@@ -456,6 +492,12 @@
             return carry
 
         lax.fori_loop(0, count, chord_up, 0)
+
+    def launch_held(v, carry):
+        launch(0, 1, v, only=by_one_link)
+        return carry
+
+    lax.fori_loop(count - held, count, launch_held, 0)
 
     with jax.named_scope("cgrad"):
         lax.fori_loop(0, count, across_gradient(0), 0)
@@ -481,20 +523,10 @@
         neighbours[2].append(jnp.where(closed_high, 0.0, above))
     interpolate(neighbours, nu)
 
-    lifts = [
-        [
-            jnp.where(low, float(HALF_LEFT[i]), jnp.where(high, float(HALF_RIGHT[i]), 0.0))
-            for i in range(5)
-        ]
-        for low, high in masks
-    ]
-    edges = [(low | high) for low, high in masks]
-    edges[0] = edges[0] & jnp.logical_not(closed)
-    full_edge = (chords == 1, spans <= 2)
+    lifts, edges = boundary_lifts(masks, closed)
 
     def outside(ref, axis, v, f):
-        value = ref[v, f]
-        return value if full_edge[axis] else jnp.where(edges[axis], value, 0.0)
+        return masked_edge(ref[v, f], axis, edges, spans)
 
     def across(axis, v):
         low, high = masks[axis]
@@ -570,34 +602,43 @@
     def correct(v, carry):
         with jax.named_scope("wait_f1"):
             await_bytes(ghosts[1][1].at[v, :, :, pl.ds(0, 2)], flux_sem.at[v])
-        flux_c, flux_s = whole(ghosts[1][0]), whole(ghosts[1][1])
-        for c in range(5):
-            along = [
-                [outside(flux_c, 0, v, 5 * b + c) for b in range(5)],
-                [outside(flux_s, 1, v, 5 * a + c) for a in range(5)],
-            ]
-            for a in range(5):
-                for b in range(5):
-                    acc[v, 25 * a + 5 * b + c] += (
-                        lifts[0][a] * along[0][b] + lifts[1][b] * along[1][a]
-                    )
+        add_fluxes(
+            lambda axis, f: outside(whole(ghosts[1][axis]), axis, v, f), lifts,
+            lambda p, value: acc.__setitem__((v, p), acc[v, p] + value),
+        )
         return carry
 
     with jax.named_scope("wait_f0"):
         await_chord(ghosts[1][0], every, chord_sem)
     with jax.named_scope("correct"):
-        lax.fori_loop(0, count, correct, 0)
+        lax.fori_loop(0, count - 1, correct, 0)
+        await_bytes(ghosts[1][1].at[count - 1, :, :, pl.ds(0, 2)], flux_sem.at[count - 1])
     with jax.named_scope("sent1"):
         all_sent(1)
 
 
-def finish_kernel(acc, nu, residual_out, nu_out, sems):
+def finish_kernel(chord_size, acc, nu, flux_c, flux_s, residual_out, nu_out, last, sems):
+    count, chords, spans, lanes = flux_c.shape[0], *flux_c.shape[2:]
+    v = count - 1
     copies = (
-        pltpu.make_async_copy(acc, residual_out, sems.at[0]),
+        pltpu.make_async_copy(acc.at[pl.ds(0, v)], residual_out.at[pl.ds(0, v)], sems.at[0]),
         pltpu.make_async_copy(nu, nu_out, sems.at[1]),
+        pltpu.make_async_copy(last, residual_out.at[v], sems.at[2]),
     )
-    for copy in copies:
-        copy.start()
+    copies[0].start()
+    copies[1].start()
+    masks = [row_masks(axis, chords, spans, lanes) for axis in range(2)]
+    closed_low, closed_high = closed_rows(chord_size, chords, spans, lanes)
+    lifts, edges = boundary_lifts(masks, closed_low | closed_high)
+    whole = [ref.reshape(count, 25, chords * spans, lanes) for ref in (flux_c, flux_s)]
+
+    def store(p, value):
+        last[p] = acc[v, p] + value
+
+    add_fluxes(
+        lambda axis, f: masked_edge(whole[axis][v, f], axis, edges, spans), lifts, store
+    )
+    copies[2].start()
     for copy in copies:
         copy.wait()
 
@@ -613,11 +654,14 @@
         return jax.ShapeDtypeStruct(shape, f32)
 
     vmem = pl.BlockSpec(memory_space=pltpu.VMEM)
-    nu, residual = pl.pallas_call(
+    faces = (count, 25, chords, spans, lanes)
+    nu, residual, flux_c, flux_s = pl.pallas_call(
         functools.partial(local_kernel, sizes, count, chords, spans),
         in_specs=[pl.BlockSpec(memory_space=pltpu.HBM)],
-        out_specs=[vmem, vmem],
-        out_shape=[full(npts, rows, lanes), full(count, npts, rows, lanes)],
+        out_specs=[vmem] * 4,
+        out_shape=[
+            full(npts, rows, lanes), full(count, npts, rows, lanes), full(*faces), full(*faces)
+        ],
         scratch_shapes=[
             pltpu.VMEM(shape, f32)
             for shape in [
@@ -628,7 +672,7 @@
                 (count, npts, rows, lanes),
                 (count, npts, rows, lanes),
             ]
-            + [(count, 25, chords, spans, lanes)] * 8
+            + [faces] * 6
         ]
         + [
             pltpu.SemaphoreType.DMA((4,)),
@@ -645,13 +689,13 @@
     )(flat)
     hbm = pl.BlockSpec(memory_space=pltpu.HBM)
     residual, nu = pl.pallas_call(
-        finish_kernel,
-        in_specs=[vmem, vmem],
+        functools.partial(finish_kernel, sizes[0]),
+        in_specs=[vmem] * 4,
         out_specs=[hbm, hbm],
         out_shape=[full(count, npts, rows, lanes), full(npts, rows, lanes)],
-        scratch_shapes=[pltpu.SemaphoreType.DMA((2,))],
+        scratch_shapes=[pltpu.VMEM((npts, rows, lanes), f32), pltpu.SemaphoreType.DMA((3,))],
         compiler_params=pltpu.CompilerParams(vmem_limit_bytes=FINISH_BYTES),
-    )(residual, nu)
+    )(residual, nu, flux_c, flux_s)
     return residual.reshape(state.shape), nu.reshape(npts, chords, spans, lanes)
 
 

time: 17.9 us -> 17.8 us (level); the launches traced: 17.8 us -> 17.5 us
  Pallas kernels: 17.1 us -> 16.8 us
    pallas_call x1, Pallas kernels: 15.5 us -> 15.2 us  [shards(): pl.pallas_call(functools.partial(local_kernel, sizes, count, chords, span...]
where the time goes in v8:
time: 17.8 us; the launch traced here: 17.5 us
  Pallas kernels  16.8 us (94%)
  between operations  0.64 us (4%)
    pallas_call x1, Pallas kernels, shards(): pl.pallas_call(functools.partial(local_kernel, sizes, count, chords, span...  15.2 us
    pallas_call x1, Pallas kernels, shards(): pl.pallas_call(functools.partial(finish_kernel, sizes[0]), in_specs=[vmem...  1.66 us

profile of v8, /device:TPU:0, one launch (start us, length us, event | category | flops | bytes accessed | tf_op | source)
XLA Modules:
  0.0 17.5 jit_solution(2939398591287853594)
XLA Ops:
  0.6 15.2 %shard_map.30 = (f32[125,8,128]{2,1,0:T(8,128)S(1)}, f32[5,125,8,128]{3,2,1,0:T(8,128)S(1)}, f32[5,25,4,2,128]{4,3,2,1,0:T(2,128)S(1)}, f32[5,25,4,2,128]{4,3,2,1,0:T(2,128)S(1)}) custom-call(f32[5,125,8,128]{3,2,1,0:T(8,128)} %bitcast.3), custom_call_target="tpu_custom_call" | custom-call | tf_op jit(solution)/shard_map/pallas_call | solution.py:658
  15.8 1.7 %shard_map.31 = (f32[5,125,8,128]{3,2,1,0:T(8,128)}, f32[125,8,128]{2,1,0:T(8,128)}) custom-call(f32[5,125,8,128]{3,2,1,0:T(8,128)S(1)} %get-tuple-element.8.acc, f32[125,8,128]{2,1,0:T(8,128)S(1)} %get-tuple-element.9.nu, f32[5,25,4,2,128]{4,3,2,1,0:T(2,128)S(1)} %get-tuple-element.10.flux_c, f32[5,25,4,2,128]{4,3,2,1,0:T(2,128)S(1)} %get-tuple-element.11.flux_s), custom_call_target="tpu_custom_call" | custom-call | tf_op jit(solution)/shard_map/pallas_call | solution.py:691

commit v9 on v8

--- a/solution.py
+++ b/solution.py
@@ -291,8 +291,6 @@
             pl.semaphore_signal(sem, inc=1, device_id=partner(dx, dy), device_id_type=mesh_id)
 
     barrier = pltpu.get_barrier_semaphore()
-    greet(barrier, level)
-
     def load(k, *part):
         return pltpu.make_async_copy(state_hbm.at[part], state.at[part], load_sem.at[k])
 
@@ -300,6 +298,8 @@
     second, others = load(2, pl.ds(1, 1)), load(3, pl.ds(2, count - 2))
     for copy in (start, remainder, second, others):
         copy.start()
+
+    greet(barrier, level)
 
     guarded(reachable(1), lambda: greet(barrier, upper))
 
@@ -331,7 +331,7 @@
     def recv_sem(stage, axis, v):
         if stage == 0:
             return state_sem.at[axis, v]
-        return chord_sem if axis == 0 else flux_sem.at[v]
+        return chord_sem if axis == 0 else flux_sem.at[jnp.where(v < count - 1, 0, 1)]
 
     def send_eps(offsets):
         for dx, dy in offsets:
@@ -600,8 +600,6 @@
         all_sent(0)
 
     def correct(v, carry):
-        with jax.named_scope("wait_f1"):
-            await_bytes(ghosts[1][1].at[v, :, :, pl.ds(0, 2)], flux_sem.at[v])
         add_fluxes(
             lambda axis, f: outside(whole(ghosts[1][axis]), axis, v, f), lifts,
             lambda p, value: acc.__setitem__((v, p), acc[v, p] + value),
@@ -611,8 +609,11 @@
     with jax.named_scope("wait_f0"):
         await_chord(ghosts[1][0], every, chord_sem)
     with jax.named_scope("correct"):
+        await_bytes(
+            ghosts[1][1].at[pl.ds(0, count - 1), :, :, pl.ds(0, 2)], flux_sem.at[0]
+        )
         lax.fori_loop(0, count - 1, correct, 0)
-        await_bytes(ghosts[1][1].at[count - 1, :, :, pl.ds(0, 2)], flux_sem.at[count - 1])
+        await_bytes(ghosts[1][1].at[count - 1, :, :, pl.ds(0, 2)], flux_sem.at[1])
     with jax.named_scope("sent1"):
         all_sent(1)
 
@@ -679,7 +680,7 @@
             pltpu.SemaphoreType.DMA((3,)),
             pltpu.SemaphoreType.DMA((2, 2)),
             pltpu.SemaphoreType.DMA((2, count)),
-            pltpu.SemaphoreType.DMA((count,)),
+            pltpu.SemaphoreType.DMA((2,)),
             pltpu.SemaphoreType.DMA,
             pltpu.SemaphoreType.REGULAR,
         ],

time: 17.8 us -> 17.7 us (level)
  no operation moved by 1% of the time
where the time goes in v9:
time: 17.7 us; the launch traced here: 17.5 us
  Pallas kernels  16.8 us (95%)
  between operations  0.64 us (4%)
    pallas_call x1, Pallas kernels, shards(): pl.pallas_call(functools.partial(local_kernel, sizes, count, chords, span...  15.2 us
    pallas_call x1, Pallas kernels, shards(): pl.pallas_call(functools.partial(finish_kernel, sizes[0]), in_specs=[vmem...  1.66 us

profile of v9, /device:TPU:0, one launch (start us, length us, event | category | flops | bytes accessed | tf_op | source)
XLA Modules:
  0.0 17.5 jit_solution(13109567534028384383)
XLA Ops:
  0.6 15.2 %shard_map.30 = (f32[125,8,128]{2,1,0:T(8,128)S(1)}, f32[5,125,8,128]{3,2,1,0:T(8,128)S(1)}, f32[5,25,4,2,128]{4,3,2,1,0:T(2,128)S(1)}, f32[5,25,4,2,128]{4,3,2,1,0:T(2,128)S(1)}) custom-call(f32[5,125,8,128]{3,2,1,0:T(8,128)} %bitcast.3), custom_call_target="tpu_custom_call" | custom-call | tf_op jit(solution)/shard_map/pallas_call | solution.py:659
  15.8 1.7 %shard_map.31 = (f32[5,125,8,128]{3,2,1,0:T(8,128)}, f32[125,8,128]{2,1,0:T(8,128)}) custom-call(f32[5,125,8,128]{3,2,1,0:T(8,128)S(1)} %get-tuple-element.8.acc, f32[125,8,128]{2,1,0:T(8,128)S(1)} %get-tuple-element.9.nu, f32[5,25,4,2,128]{4,3,2,1,0:T(2,128)S(1)} %get-tuple-element.10.flux_c, f32[5,25,4,2,128]{4,3,2,1,0:T(2,128)S(1)} %get-tuple-element.11.flux_s), custom_call_target="tpu_custom_call" | custom-call | tf_op jit(solution)/shard_map/pallas_call | solution.py:692

commit v10 on v9

--- a/solution.py
+++ b/solution.py
@@ -295,8 +295,8 @@
         return pltpu.make_async_copy(state_hbm.at[part], state.at[part], load_sem.at[k])
 
     start, remainder = load(0, 0, pl.ds(0, 75)), load(1, 0, pl.ds(75, 50))
-    second, others = load(2, pl.ds(1, 1)), load(3, pl.ds(2, count - 2))
-    for copy in (start, remainder, second, others):
+    others = load(2, pl.ds(1, count - 1))
+    for copy in (start, remainder, others):
         copy.start()
 
     greet(barrier, level)
@@ -346,7 +346,7 @@
                 pltpu.make_async_remote_copy(
                     src_ref=side(faces[stage][axis], axis, v, up, part),
                     dst_ref=side(ghosts[stage][axis], axis, v, not up, part),
-                    send_sem=send_sem.at[stage, axis], recv_sem=recv_sem(stage, axis, v),
+                    send_sem=send_sem.at[stage if axis == 0 else 2], recv_sem=recv_sem(stage, axis, v),
                     device_id=partner(dx, dy), device_id_type=mesh_id,
                 ).start()
 
@@ -383,8 +383,9 @@
     every = pl.ds(0, count)
 
     def all_sent(stage):
-        await_chord(faces[stage][0], every, send_sem.at[stage, 0])
-        await_bytes(faces[stage][1].at[:, :, :, pl.ds(0, 2)], send_sem.at[stage, 1])
+        await_chord(faces[stage][0], every, send_sem.at[stage])
+        if stage == 1:
+            await_bytes(state.at[:, pl.ds(0, 100 // spans)], send_sem.at[2])
 
     masks = [row_masks(axis, chords, spans, lanes) for axis in range(2)]
 
@@ -420,10 +421,8 @@
             return carry
 
         held = min(HELD, count - 1)
-        second.wait()
-        span_traces(1, 0)
         others.wait()
-        lax.fori_loop(2, count, span_traces, 0)
+        lax.fori_loop(1, count, span_traces, 0)
 
         def chord_traces(v, carry):
             form_traces(0, v)
@@ -676,9 +675,9 @@
             + [faces] * 6
         ]
         + [
-            pltpu.SemaphoreType.DMA((4,)),
             pltpu.SemaphoreType.DMA((3,)),
-            pltpu.SemaphoreType.DMA((2, 2)),
+            pltpu.SemaphoreType.DMA((3,)),
+            pltpu.SemaphoreType.DMA((3,)),
             pltpu.SemaphoreType.DMA((2, count)),
             pltpu.SemaphoreType.DMA((2,)),
             pltpu.SemaphoreType.DMA,

time: 17.7 us -> 17.8 us (level)
  no operation moved by 1% of the time
where the time goes in v10:
time: 17.8 us; the launch traced here: 17.6 us
  Pallas kernels  16.9 us (95%)
  between operations  0.64 us (4%)
    pallas_call x1, Pallas kernels, shards(): pl.pallas_call(functools.partial(local_kernel, sizes, count, chords, span...  15.3 us
    pallas_call x1, Pallas kernels, shards(): pl.pallas_call(functools.partial(finish_kernel, sizes[0]), in_specs=[vmem...  1.66 us

profile of v10, /device:TPU:0, one launch (start us, length us, event | category | flops | bytes accessed | tf_op | source)
XLA Modules:
  0.0 17.6 jit_solution(12688112749910399958)
XLA Ops:
  0.6 15.3 %shard_map.30 = (f32[125,8,128]{2,1,0:T(8,128)S(1)}, f32[5,125,8,128]{3,2,1,0:T(8,128)S(1)}, f32[5,25,4,2,128]{4,3,2,1,0:T(2,128)S(1)}, f32[5,25,4,2,128]{4,3,2,1,0:T(2,128)S(1)}) custom-call(f32[5,125,8,128]{3,2,1,0:T(8,128)} %bitcast.3), custom_call_target="tpu_custom_call" | custom-call | tf_op jit(solution)/shard_map/pallas_call | solution.py:658
  15.9 1.7 %shard_map.31 = (f32[5,125,8,128]{3,2,1,0:T(8,128)}, f32[125,8,128]{2,1,0:T(8,128)}) custom-call(f32[5,125,8,128]{3,2,1,0:T(8,128)S(1)} %get-tuple-element.8.acc, f32[125,8,128]{2,1,0:T(8,128)S(1)} %get-tuple-element.9.nu, f32[5,25,4,2,128]{4,3,2,1,0:T(2,128)S(1)} %get-tuple-element.10.flux_c, f32[5,25,4,2,128]{4,3,2,1,0:T(2,128)S(1)} %get-tuple-element.11.flux_s), custom_call_target="tpu_custom_call" | custom-call | tf_op jit(solution)/shard_map/pallas_call | solution.py:691
